TPU v7x, 32 devices: a whole 2x2x4 slice. The times are simulated.
32 devices in a mesh: slab: 8 (over z, y), md: 4 (over x, core).
Axes of the slice: x: 2, y: 2, z: 4, core: 2. Of those that a mesh axis runs over, the one named last changes fastest.
Arguments:
- populations: float32 [19, 16, 256, 128], P(None, 'slab', 'md'), may hold values from 0.02 to 0.1
- relax: float32 [16, 256, 128], P('slab', 'md'), may hold values from 0.8 to 1.8
- owners: int32 [16, 256, 2], P('slab', 'md'), may hold values from 0 to 31, all different within a row; in each aligned block of 64 rows (0 to 63, 64 to 127, ..., all dimensions but the last counted through in order) at most 8 rows name the same one
- positions: float32 [3, 32768], P(None, ('slab', 'md')), may hold values from 0 to 3
- velocities: float32 [3, 32768], P(None, ('slab', 'md')), may hold values from -5 to 5
- neighbours: int32 [32768, 64], P(('slab', 'md')), may hold values from 0 to 1023
- atom_slots: int32 [32768], P(('slab', 'md')), may hold values from 0 to 511
Outputs:
- populations_out: float32 [19, 16, 256, 128], P(None, 'slab', 'md')
- positions_out: float32 [3, 32768], P(None, ('slab', 'md'))
- velocities_out: float32 [3, 32768], P(None, ('slab', 'md'))
- cell_moments: float32 [4, 16, 256], P(None, 'slab', 'md')
Inputs may be any that keep to these rules, and one draw needn't show every extreme that they name: The 64 entries of one z position on one device name any owner at most 8 times in each column k and across k; the 2 owners of one cell differ. `neighbours`: entries index atoms of the same subdomain's block of 1024 atoms; an atom that lists itself is padding.
All inputs are finite; a program needn't handle non-finite values.
Results may differ from a plain program's by a relative error of at most 0.0003.
Values sent between devices are 32-bit elements; how exact they have to be, the bound alone decides.
A program may use at most 64 MiB of HBM per device.

v0:
```python
import functools

import jax
import jax.numpy as jnp
from jax import lax
from jax.experimental import pallas as pl
from jax.experimental.pallas import tpu as pltpu
from jax.sharding import PartitionSpec as P

LB_STEPS = 4
MD_STEPS = 5

ORDER = [13, 1, 7, 9, 11, 5, 15, 18, 14, 2, 8, 10, 12, 6, 16, 17, 0, 3, 4]
lattice_dirs = [
    (0, 0, 0),
    (1, 0, 0),
    (-1, 0, 0),
    (0, 1, 0),
    (0, -1, 0),
    (0, 0, 1),
    (0, 0, -1),
    (1, 1, 0),
    (-1, -1, 0),
    (1, -1, 0),
    (-1, 1, 0),
    (1, 0, 1),
    (-1, 0, -1),
    (1, 0, -1),
    (-1, 0, 1),
    (0, 1, 1),
    (0, -1, -1),
    (0, 1, -1),
    (0, -1, 1),
]
DIRS = [lattice_dirs[i] for i in ORDER]
velocity_scale = 10.0
pair_strength = 0.5
friction = 2.0
time_step = 0.1
MESH = pl.DeviceIdType.MESH


def total_of(terms):
    terms = list(terms)
    while len(terms) > 1:
        terms = [a + b for a, b in zip(terms[::2], terms[1::2])] + (
            [terms[-1]] if len(terms) % 2 else []
        )
    return terms[0]


def fields(f):
    density = total_of(f)
    inverse = 1.0 / density
    vel = []
    for axis in range(3):
        plus = total_of(f[p] for p in range(19) if DIRS[p][axis] == 1)
        minus = total_of(f[p] for p in range(19) if DIRS[p][axis] == -1)
        vel.append((plus - minus) * inverse)
    return density, vel


def collided(f, relax):
    density, (vx, vy, vz) = fields(f)
    base = 1.0 - 1.5 * (vx * vx + vy * vy + vz * vz)
    keep = 1.0 - relax
    scale = relax * density
    result = [None] * 19
    for p, c in enumerate(DIRS):
        if result[p] is not None:
            continue
        size = sum(abs(e) for e in c)
        if size == 0:
            result[p] = keep * f[p] + (scale * (1.0 / 3.0)) * base
            continue
        along = total_of(v if e == 1 else -v for e, v in zip(c, (vx, vy, vz)) if e)
        weight = scale * (1.0 / 18.0 if size == 1 else 1.0 / 36.0)
        even = weight * (base + 4.5 * (along * along))
        odd = weight * (3.0 * along)
        q = DIRS.index(tuple(-e for e in c))
        result[p] = keep * f[p] + (even + odd)
        result[q] = keep * f[q] + (even - odd)
    return result


def lane_gather(table, index):
    return jnp.take_along_axis(table, index, axis=1, mode="promise_in_bounds")


def thirds(value):
    parts = []
    for _ in range(3):
        piece = value.astype(jnp.bfloat16).astype(jnp.float32)
        parts.append(piece)
        value = value - piece
    return parts


def by_hits(data, hits, dims):
    return lax.dot_general(
        data.astype(jnp.bfloat16), hits, (dims, ((), ())), preferred_element_type=jnp.float32
    )


def coupled_kernel(
    n_slab,
    n_md,
    f_ref,
    relax_ref,
    own_ref,
    pos_ref,
    vel_ref,
    nbr_ref,
    slots_ref,
    out_ref,
    pos_out,
    vel_out,
    cell_out,
    post,
    rows_out,
    rows_in,
    mean_ref,
    at,
    pull,
    data,
    hits,
    placed,
    tgt,
    table,
    blocks_out,
    blocks_in,
    send,
    recv,
    swap_send,
    swap_recv,
):
    cz, cx, ny = relax_ref.shape
    top_z = cz - 1
    cells = cz * cx
    entries, atoms = nbr_ref.shape
    groups = atoms // 128
    slot_count = hits.shape[0]
    devices = n_slab * n_md
    cap = slot_count // devices
    slab, md = lax.axis_index("slab"), lax.axis_index("md")
    me = slab * n_md + md
    above, below = lax.rem(slab + 1, n_slab), lax.rem(slab + n_slab - 1, n_slab)
    right, left = lax.rem(md + 1, n_md), lax.rem(md + n_md - 1, n_md)
    barrier = pltpu.get_barrier_semaphore()

    def coords(device):
        return (lax.div(device, n_md), lax.rem(device, n_md))

    def greet(k, carry):
        peer = coords(lax.rem(me + k, devices))
        pl.semaphore_signal(barrier, inc=1, device_id=peer, device_id_type=MESH)
        return carry

    lax.fori_loop(1, devices, greet, 0)

    def load(step, z, x0):
        if step == 0:
            return [f_ref[ORDER[p], z, pl.ds(x0, 8), :] for p in range(19)]
        return [
            post[step - 1, p, z + 1 - c[2], pl.ds(x0 + (8 - c[0]), 8), :]
            for p, c in enumerate(DIRS)
        ]

    def plane(step, z):
        def block(b, carry):
            x0 = pl.multiple_of(b * 8, 8)
            done = collided(load(step, z, x0), relax_ref[z, pl.ds(x0, 8), :])
            for p, c in enumerate(DIRS):
                value = done[p] if c[1] == 0 else pltpu.roll(done[p], c[1] % ny, axis=1)
                post[step, p, z + 1, pl.ds(x0 + 8, 8), :] = value
            return carry

        lax.fori_loop(0, cx // 8, block, 0, unroll=2)
        for side, first, row in ((0, 0, 7 + cx), (1, 8, 8)):
            for j in range(5):
                rows_out[step, z, side, j, :] = post[step, first + j, z + 1, row, :]

    copies = []

    def copy(step, slot, src, dst, peer):
        made = pltpu.make_async_remote_copy(
            src_ref=src,
            dst_ref=dst,
            send_sem=send.at[step, slot],
            recv_sem=recv.at[step, slot],
            device_id=peer,
            device_id_type=MESH,
        )
        made.start()
        copies.append(made)
        return made

    own = pl.ds(8, cx)

    def send_rows(step, z):
        return [
            copy(
                step,
                7 + 2 * z + side,
                rows_out.at[step, z, side],
                rows_in.at[step, z + 1, side],
                (slab, (right, left)[side]),
            )
            for side in range(2)
        ]

    def send_z(step, rising):
        z, slot, peer = (top_z, 0, above) if rising else (0, cz + 1, below)
        base = 0 if rising else 3
        made = [
            copy(
                step,
                base + 1 + side,
                rows_out.at[step, z, side],
                rows_in.at[step, slot, side],
                (peer, (right, left)[side]),
            )
            for side in range(2)
        ]
        spans = ((4, 5, 0),) if rising else ((12, 4, 3), (0, 1, 6))
        for first, count, sem in spans:
            made.append(
                copy(
                    step,
                    sem,
                    post.at[step, pl.ds(first, count), z + 1, own, :],
                    post.at[step, pl.ds(first, count), slot, own, :],
                    (peer, md),
                )
            )
        return made

    def arrive(made):
        for one in made:
            one.wait_recv()

    def put_rows(step):
        for z in range(cz):
            for side, first, row in ((0, 0, 7), (1, 8, 8 + cx)):
                for j in range(5):
                    post[step, first + j, z + 1, row, :] = rows_in[step, z + 1, side, j, :]

    def put_corners(step, rising):
        slot = 0 if rising else cz + 1
        for side, row in ((0, 7), (1, 8 + cx)):
            j = (4, 0)[side] if rising else (0, 4)[side]
            post[step, 8 * side + j, slot, row, :] = rows_in[step, slot, side, j, :]

    def pair_forces():
        def one_group(g, inner):
            mine = [jnp.broadcast_to(at[c, pl.ds(g, 1), :], (8, 128)) for c in range(3)]
            sums = [jnp.zeros((8, 128), jnp.float32)] * 3
            for k in range(0, entries, 8):
                index = nbr_ref[pl.ds(k, 8), pl.ds(pl.multiple_of(g * 128, 128), 128)]
                lane, row = index & 127, index >> 7
                found = [None] * 3
                for h in range(groups):
                    pick = row == h
                    for c in range(3):
                        line = jnp.broadcast_to(at[c, pl.ds(h, 1), :], (8, 128))
                        value = lane_gather(line, lane)
                        found[c] = value if h == 0 else jnp.where(pick, value, found[c])
                gap = [found[c] - mine[c] for c in range(3)]
                weight = jnp.exp(-0.5 * (gap[0] * gap[0] + gap[1] * gap[1] + gap[2] * gap[2]))
                sums = [sums[c] + gap[c] * weight for c in range(3)]
            for c in range(3):
                pull[c, pl.ds(g, 1), :] = jnp.sum(sums[c], axis=0, keepdims=True)
            return inner

        lax.fori_loop(0, groups, one_group, 0)

    def prepare_particles():
        for g in range(groups):
            here = pl.ds(g * 128, 128)
            for c in range(3):
                at[c, pl.ds(g, 1), :] = pos_ref[pl.ds(c, 1), here]
                at[3 + c, pl.ds(g, 1), :] = vel_ref[pl.ds(c, 1), here]
        pair_forces()

    def prepare_hits():
        data[...] = jnp.ones(data.shape, jnp.float32)
        tgt[...] = jnp.zeros(tgt.shape, jnp.float32)
        table[...] = jnp.zeros(table.shape, jnp.float32)
        for g in range(groups):
            label = lax.broadcasted_iota(jnp.int32, (slot_count, 128), 0)
            same = label == slots_ref[pl.ds(g, 1), :]
            hits[:, pl.ds(g * 128, 128)] = jnp.where(same, 1.0, 0.0).astype(jnp.bfloat16)

    def prepare_routes():
        top = own_ref.shape[0]
        label = lax.broadcasted_iota(jnp.int32, (devices, cells), 0)
        owned = [jnp.where(label == own_ref[pl.ds(k, 1), :], 1.0, 0.0) for k in range(top)]
        earlier = lax.broadcasted_iota(jnp.int32, (cells, cells), 0) < lax.broadcasted_iota(
            jnp.int32, (cells, cells), 1
        )
        before = by_hits(
            total_of(owned), jnp.where(earlier, 1.0, 0.0).astype(jnp.bfloat16), ((1,), (0,))
        )
        start = (label * cap).astype(jnp.float32)
        place = lax.broadcasted_iota(jnp.int32, (slot_count, cells), 0).astype(jnp.float32)
        filled = jnp.zeros((slot_count, cells), jnp.float32)
        for k in range(top):
            spot = jnp.sum((before + start) * owned[k], axis=0, keepdims=True)
            filled = filled + jnp.where(place == spot, 1.0, 0.0)
            before = before + owned[k]
        placed[...] = filled.astype(jnp.bfloat16)

    def swap(turn, values):
        per = 128 // cap
        for d in range(devices):
            chunk = values[:, d // per * 128 : (d // per + 1) * 128]
            shift = (128 - d % per * cap) % 128
            blocks_out[turn, d] = chunk if shift == 0 else pltpu.roll(chunk, shift, axis=1)

        def trade(k):
            to = lax.rem(me + k, devices)
            return pltpu.make_async_remote_copy(
                src_ref=blocks_out.at[turn, to],
                dst_ref=blocks_in.at[turn, me],
                send_sem=swap_send.at[turn, k],
                recv_sem=swap_recv.at[turn, k],
                device_id=coords(to),
                device_id_type=MESH,
            )

        def begin(k, carry):
            trade(k).start()
            return carry

        def landed(k, carry):
            origin = lax.rem(me + devices - k, devices)
            pltpu.make_async_remote_copy(
                src_ref=blocks_out.at[turn, origin],
                dst_ref=blocks_in.at[turn, origin],
                send_sem=swap_send.at[turn, k],
                recv_sem=swap_recv.at[turn, k],
                device_id=coords(origin),
                device_id_type=MESH,
            ).wait_recv()
            return carry

        def sent(k, carry):
            trade(k).wait_send()
            return carry

        lax.fori_loop(1, devices, begin, 0)
        blocks_in[turn, me] = blocks_out[turn, me]
        lax.fori_loop(1, devices, landed, 0)
        zone = lax.broadcasted_iota(jnp.int32, (4, 128), 1) // cap
        lines = []
        for h in range(slot_count // 128):
            line = jnp.zeros((4, 128), jnp.float32)
            for j in range(per):
                value = blocks_in[turn, h * per + j]
                if j:
                    value = pltpu.roll(value, j * cap, axis=1)
                line = jnp.where(zone == j, value, line)
            lines.append(line)
        return lines, lambda: lax.fori_loop(1, devices, sent, 0)

    last = {}
    plane(0, 0)
    for z in range(1, top_z):
        plane(0, z)
    pl.semaphore_wait(barrier, devices - 1)
    rows = []
    for z in range(top_z):
        rows += send_rows(0, z)
    last[False] = send_z(0, False)
    plane(0, top_z)
    rows += send_rows(0, top_z)
    last[True] = send_z(0, True)
    prepare_particles()
    for step in range(1, LB_STEPS):
        arrive(rows)
        put_rows(step - 1)
        rows, coming = [], {}
        for rising in ((False, True), (True, False))[(step + 1) % 2]:
            arrive(last[rising])
            put_corners(step - 1, rising)
            levels = range(top_z) if rising else [top_z]
            for z in levels:
                plane(step, z)
                rows += send_rows(step, z)
            coming[not rising] = send_z(step, not rising)
        last = coming
        if step == 1:
            prepare_hits()
        if step == 2:
            prepare_routes()
    arrive(rows)
    put_rows(LB_STEPS - 1)
    for rising in ((False, True), (True, False))[(LB_STEPS + 1) % 2]:
        arrive(last[rising])
        put_corners(LB_STEPS - 1, rising)
        for z in range(top_z) if rising else [top_z]:

            def finish(b, carry, z=z):
                x0 = pl.multiple_of(b * 8, 8)
                f = load(LB_STEPS, z, x0)
                for p in range(19):
                    out_ref[ORDER[p], z, pl.ds(x0, 8), :] = f[p]
                density, vel = fields(f)
                for c, value in enumerate((*vel, density)):
                    mean_ref[c, pl.ds(x0 + z * cx, 8), :] = value
                return carry

            lax.fori_loop(0, cx // 8, finish, 0, unroll=2)
    for c in range(4):
        scale = (velocity_scale if c < 3 else 1.0) / ny
        mean = jnp.sum(mean_ref[c].T, axis=0, keepdims=True) * scale
        for part, piece in enumerate(thirds(mean)):
            tgt[pl.ds(part * 4 + c, 1), :] = piece
    sums = by_hits(tgt[...], placed[...], ((1,), (1,)))
    lines, sent_first = swap(0, sums[0:4] + sums[4:8] + sums[8:12])

    slots = slots_ref[...]
    lane, row = slots & 127, slots >> 7
    goal = []
    for c in range(4):
        value = jnp.zeros((groups, 128), jnp.float32)
        for h, line in enumerate(lines):
            spread = jnp.broadcast_to(line[c : c + 1, :], (groups, 128))
            value = jnp.where(row == h, lane_gather(spread, lane), value)
        goal.append(value)
    rate = friction * goal[3]

    def advance():
        for c in range(3):
            vel = at[3 + c]
            force = pair_strength * pull[c] + rate * (goal[c] - vel)
            vel = vel + time_step * force
            at[3 + c] = vel
            at[c] = at[c] + time_step * vel

    def one_step(step, carry):
        pair_forces()
        advance()
        return carry

    advance()
    lax.fori_loop(1, MD_STEPS, one_step, 0)
    at[6] = at[3] * at[3] + at[4] * at[4] + at[5] * at[5]
    for c in range(4):
        for part, piece in enumerate(thirds(at[3 + c])):
            for g in range(groups):
                data[pl.ds(part * 4 + c, 1), pl.ds(g * 128, 128)] = piece[g : g + 1, :]
    sums = by_hits(data[...], hits[...], ((1,), (1,)))
    moments = (sums[0:4] + sums[4:8] + sums[8:12]) / jnp.maximum(sums[12:13], 1.0)
    lines, sent_second = swap(1, moments)
    for h, line in enumerate(lines):
        for part, piece in enumerate(thirds(line)):
            table[pl.ds(part * 4, 4), pl.ds(h * 128, 128)] = piece
    sums = by_hits(table[...], placed[...], ((1,), (0,)))
    picked = sums[0:4] + sums[4:8] + sums[8:12]
    for c in range(4):
        for z in range(cz):
            cell_out[c, pl.ds(z, 1), :] = picked[c : c + 1, z * cx : (z + 1) * cx]
    for g in range(groups):
        here = pl.ds(g * 128, 128)
        for c in range(3):
            pos_out[pl.ds(c, 1), here] = at[c, pl.ds(g, 1), :]
            vel_out[pl.ds(c, 1), here] = at[3 + c, pl.ds(g, 1), :]
    sent_first()
    sent_second()
    for made in copies:
        made.wait_send()


def on_device(populations, relax, owners, positions, velocities, neighbours, atom_slots):
    cz, cx, ny = relax.shape
    n_slab = lax.axis_size("slab")
    n_md = lax.axis_size("md")
    devices = n_slab * n_md
    top = owners.shape[2]
    cap = cz * max(2, 2 * cx * top // devices)
    slots = devices * cap
    atoms, entries = neighbours.shape
    groups = atoms // 128
    cells = cz * cx
    vmem = pl.BlockSpec(memory_space=pltpu.VMEM)
    dma = pltpu.SemaphoreType.DMA
    return pl.pallas_call(
        functools.partial(coupled_kernel, n_slab, n_md),
        out_shape=(
            jax.ShapeDtypeStruct(populations.shape, jnp.float32),
            jax.ShapeDtypeStruct(positions.shape, jnp.float32),
            jax.ShapeDtypeStruct(velocities.shape, jnp.float32),
            jax.ShapeDtypeStruct((4, cz, cx), jnp.float32),
        ),
        in_specs=[vmem] * 7,
        out_specs=(vmem,) * 4,
        scratch_shapes=[
            pltpu.VMEM((LB_STEPS, 19, cz + 2, cx + 16, ny), jnp.float32),
            pltpu.VMEM((LB_STEPS, cz, 2, 8, ny), jnp.float32),
            pltpu.VMEM((LB_STEPS, cz + 2, 2, 8, ny), jnp.float32),
            pltpu.VMEM((4, cells, ny), jnp.float32),
            pltpu.VMEM((7, groups, 128), jnp.float32),
            pltpu.VMEM((3, groups, 128), jnp.float32),
            pltpu.VMEM((16, atoms), jnp.float32),
            pltpu.VMEM((slots, atoms), jnp.bfloat16),
            pltpu.VMEM((slots, cells), jnp.bfloat16),
            pltpu.VMEM((16, cells), jnp.float32),
            pltpu.VMEM((16, slots), jnp.float32),
            pltpu.VMEM((2, devices, 4, 128), jnp.float32),
            pltpu.VMEM((2, devices, 4, 128), jnp.float32),
            dma((LB_STEPS, 7 + 2 * cz)),
            dma((LB_STEPS, 7 + 2 * cz)),
            dma((2, devices)),
            dma((2, devices)),
        ],
        compiler_params=pltpu.CompilerParams(
            collective_id=0, has_side_effects=True, vmem_limit_bytes=40 * 1024 * 1024
        ),
        name="coupled",
    )(
        populations,
        relax,
        owners.reshape(cells, top).T,
        positions,
        velocities,
        neighbours.T,
        atom_slots.reshape(groups, 128),
    )


def solution(mesh):
    return jax.shard_map(
        on_device,
        mesh=mesh,
        in_specs=(
            P(None, "slab", "md", None),
            P("slab", "md", None),
            P("slab", "md", None),
            P(None, ("slab", "md")),
            P(None, ("slab", "md")),
            P(("slab", "md"), None),
            P(("slab", "md")),
        ),
        out_specs=(
            P(None, "slab", "md", None),
            P(None, ("slab", "md")),
            P(None, ("slab", "md")),
            P(None, "slab", "md"),
        ),
        check_vma=False,
    )
```

profile of v0, /device:TPU:0, one launch (start us, length us, event | category | flops | bytes accessed | tf_op | source)
XLA Modules:
  0.0 80.5 jit_solution(10505898451155002427)
XLA Ops:
  0.6 0.7 copy.11
  1.3 0.1 reshape.14
  1.4 0.0 copy-start
  1.4 1.3 %copy-done = f32[19,2,64,128]{3,2,1,0:T(8,128)S(1)} copy-done((f32[19,2,64,128]{3,2,1,0:T(8,128)S(1)}, f32[19,2,64,128]{3,2,1,0:T(8,128)}, u32[]{:S(2)}) %copy-start) | copy-done | bytes 1245208
  2.7 0.0 copy-start.1
  2.7 0.9 %copy-done.1 = s32[1024,64]{0,1:T(8,128)S(1)} copy-done((s32[1024,64]{0,1:T(8,128)S(1)}, s32[1024,64]{0,1:T(8,128)}, u32[]{:S(2)}) %copy-start.1) | copy-done | bytes 262168
  3.6 0.0 copy-start.2
  3.6 0.8 %copy-done.2 = f32[2,64,128]{2,1,0:T(8,128)S(1)} copy-done((f32[2,64,128]{2,1,0:T(8,128)S(1)}, f32[2,64,128]{2,1,0:T(8,128)}, u32[]{:S(2)}) %copy-start.2) | copy-done | bytes 65560
  4.5 0.0 copy-start.3
  4.5 0.7 copy-done.3
  5.2 0.0 copy-start.4
  5.2 0.7 copy-done.4
  5.9 0.0 copy-start.5
  5.9 0.7 copy-done.5
  6.6 71.0 %coupled.1 = (f32[19,2,64,128]{3,2,1,0:T(8,128)S(1)}, f32[3,1024]{1,0:T(4,128)S(1)}, f32[3,1024]{1,0:T(4,128)S(1)}, f32[4,2,64]{2,1,0:T(2,128)S(1)}) custom-call(f32[19,2,64,128]{3,2,1,0:T(8,128)S(1)} %copy-done, f32[2,64,128]{2,1,0:T(8,128)S(1)} %copy-done.2, s32[2,128]{1,0:T(2,128)S(1)} %bitcast.7, f32[3,1024]{1,0:T(4,128)S(1)} %copy-done.3, ...), custom_call_target="tpu_custom_call" | custom-call | tf_op jit(solution)/shard_map/coupled/pallas_call | solution.py:488
  77.6 1.0 %copy.16 = f32[19,2,64,128]{3,2,1,0:T(8,128)} copy(f32[19,2,64,128]{3,2,1,0:T(8,128)S(1)} %get-tuple-element.8) | data formatting | bytes 2490368
  78.7 0.6 copy.17
  79.3 0.6 copy.18
  79.9 0.6 copy.19
Async XLA Ops:
  1.4 1.3 %copy-start = (f32[19,2,64,128]{3,2,1,0:T(8,128)S(1)}, f32[19,2,64,128]{3,2,1,0:T(8,128)}, u32[]{:S(2)}) copy-start(f32[19,2,64,128]{3,2,1,0:T(8,128)} %f_ref.1) | copy-start | bytes 3735556
  2.7 0.9 %copy-start.1 = (s32[1024,64]{0,1:T(8,128)S(1)}, s32[1024,64]{0,1:T(8,128)}, u32[]{:S(2)}) copy-start(s32[1024,64]{0,1:T(8,128)} %param.12) | copy-start | bytes 786436
  3.6 0.8 %copy-start.2 = (f32[2,64,128]{2,1,0:T(8,128)S(1)}, f32[2,64,128]{2,1,0:T(8,128)}, u32[]{:S(2)}) copy-start(f32[2,64,128]{2,1,0:T(8,128)} %relax_ref.1) | copy-start | bytes 196612
  4.5 0.7 copy-start.3
  5.2 0.7 copy-start.4
  5.9 0.7 copy-start.5
where the time goes:
time: 80.9 us; the launch traced here: 80.5 us
  Pallas kernels  71 us (88%)
  local copies, waits for them, and re-layouts  8.81 us (11%)
    pallas_call x1, Pallas kernels, on_device(): pl.pallas_call(functools.partial(coupled_kernel, n_slab, n_md), out_shape...  71 us
    unnamed x17, local copies, waits for them, and re-layouts  8.72 us

commit v1 on v0

v1 whole, which is shorter than its diff:
```python
import contextlib
import functools

import jax
import jax.numpy as jnp
from jax import lax
from jax.experimental import pallas as pl
from jax.experimental.pallas import tpu as pltpu
from jax.sharding import PartitionSpec as P

LB_STEPS = 4
MD_STEPS = 5

ORDER = [11, 14, 5, 15, 18, 12, 13, 6, 16, 17, 0, 1, 2, 3, 4, 7, 8, 9, 10]
lattice_dirs = [
    (0, 0, 0),
    (1, 0, 0),
    (-1, 0, 0),
    (0, 1, 0),
    (0, -1, 0),
    (0, 0, 1),
    (0, 0, -1),
    (1, 1, 0),
    (-1, -1, 0),
    (1, -1, 0),
    (-1, 1, 0),
    (1, 0, 1),
    (-1, 0, -1),
    (1, 0, -1),
    (-1, 0, 1),
    (0, 1, 1),
    (0, -1, -1),
    (0, 1, -1),
    (0, -1, 1),
]
DIRS = [lattice_dirs[i] for i in ORDER]
FACES = [[p for p in range(19) if DIRS[p][0] == 1], [p for p in range(19) if DIRS[p][0] == -1]]
velocity_scale = 10.0
pair_strength = 0.5
friction = 2.0
time_step = 0.1
MESH = pl.DeviceIdType.MESH


def parts_of(cx):
    edges = list(range(0, cx + 1, 8))
    parts = list(zip(edges[:-1], edges[1:]))
    order = []
    while parts:
        order.append(parts.pop(0))
        if parts:
            order.append(parts.pop())
    return order


def mark(name):
    return contextlib.nullcontext()


def total_of(terms):
    terms = list(terms)
    while len(terms) > 1:
        terms = [a + b for a, b in zip(terms[::2], terms[1::2])] + (
            [terms[-1]] if len(terms) % 2 else []
        )
    return terms[0]


def fields(f):
    density = total_of(f)
    inverse = 1.0 / density
    vel = []
    for axis in range(3):
        plus = total_of(f[p] for p in range(19) if DIRS[p][axis] == 1)
        minus = total_of(f[p] for p in range(19) if DIRS[p][axis] == -1)
        vel.append((plus - minus) * inverse)
    return density, vel


def collided(f, relax):
    density, (vx, vy, vz) = fields(f)
    base = 1.0 - 1.5 * (vx * vx + vy * vy + vz * vz)
    keep = 1.0 - relax
    scale = relax * density
    result = [None] * 19
    for p, c in enumerate(DIRS):
        if result[p] is not None:
            continue
        size = sum(abs(e) for e in c)
        if size == 0:
            result[p] = keep * f[p] + (scale * (1.0 / 3.0)) * base
            continue
        along = total_of(v if e == 1 else -v for e, v in zip(c, (vx, vy, vz)) if e)
        weight = scale * (1.0 / 18.0 if size == 1 else 1.0 / 36.0)
        even = weight * (base + 4.5 * (along * along))
        odd = weight * (3.0 * along)
        q = DIRS.index(tuple(-e for e in c))
        result[p] = keep * f[p] + (even + odd)
        result[q] = keep * f[q] + (even - odd)
    return result


def lane_gather(table, index):
    return jnp.take_along_axis(table, index, axis=1, mode="promise_in_bounds")


def thirds(value):
    parts = []
    for _ in range(3):
        piece = value.astype(jnp.bfloat16).astype(jnp.float32)
        parts.append(piece)
        value = value - piece
    return parts


def by_hits(data, hits, dims):
    return lax.dot_general(
        data.astype(jnp.bfloat16), hits, (dims, ((), ())), preferred_element_type=jnp.float32
    )


def coupled_kernel(
    n_slab,
    n_md,
    f_hbm,
    relax_hbm,
    own_hbm,
    pos_hbm,
    vel_hbm,
    nbr_hbm,
    slots_hbm,
    out_ref,
    pos_out,
    vel_out,
    cell_out,
    f_ref,
    relax_ref,
    own_ref,
    pos_ref,
    vel_ref,
    nbr_ref,
    slots_ref,
    load_sem,
    post,
    rows_out,
    rows_in,
    mean_ref,
    at,
    pull,
    data,
    hits,
    placed,
    tgt,
    table,
    blocks_out,
    blocks_in,
    send,
    recv,
    swap_send,
    swap_recv,
):
    cz, cx, ny = relax_ref.shape
    top_z = cz - 1
    cells = cz * cx
    entries, atoms = nbr_ref.shape
    groups = atoms // 128
    slot_count = hits.shape[0]
    devices = n_slab * n_md
    cap = slot_count // devices
    parts = parts_of(cx)
    chunks = len(parts)
    outer = [[low for low, _ in parts].index(0), [high for _, high in parts].index(cx)]
    slab, md = lax.axis_index("slab"), lax.axis_index("md")
    me = slab * n_md + md

    def wrapped(value, size):
        return jnp.where(value >= size, value - size, value)

    above, below = wrapped(slab + 1, n_slab), wrapped(slab + n_slab - 1, n_slab)
    right, left = wrapped(md + 1, n_md), wrapped(md + n_md - 1, n_md)
    barrier = pltpu.get_barrier_semaphore()

    def peer_of(k):
        return wrapped(slab + k // n_md, n_slab), wrapped(md + k % n_md, n_md)

    def source_of(k):
        return wrapped(slab + n_slab - k // n_md, n_slab), wrapped(md + n_md - k % n_md, n_md)

    for k in range(1, devices):
        pl.semaphore_signal(barrier, inc=1, device_id=peer_of(k), device_id_type=MESH)

    loads = []

    def fetch(src, dst):
        made = pltpu.make_async_copy(src, dst, load_sem.at[len(loads)])
        made.start()
        loads.append(made)
        return made

    f_parts = []
    for low, high in parts:
        here = pl.ds(low, high - low)
        f_parts.append(fetch(f_hbm.at[:, :, here, :], f_ref.at[:, :, here, :]))
        if len(f_parts) == 1:
            relax_part = fetch(relax_hbm, relax_ref)
    pos_parts = [fetch(pos_hbm, pos_ref), fetch(vel_hbm, vel_ref), fetch(nbr_hbm, nbr_ref)]
    slots_part = fetch(slots_hbm, slots_ref)
    own_part = fetch(own_hbm, own_ref)

    def load(step, z, x0):
        if step == 0:
            return [f_ref[ORDER[p], z, pl.ds(x0, 8), :] for p in range(19)]
        return [
            post[step - 1, p, z + 1 - c[2], pl.ds(x0 + (8 - c[0]), 8), :]
            for p, c in enumerate(DIRS)
        ]

    def collide_chunk(step, z, part):
        for x0 in range(*parts[part], 8):
            done = collided(load(step, z, x0), relax_ref[z, pl.ds(x0, 8), :])
            for p, c in enumerate(DIRS):
                value = done[p] if c[1] == 0 else pltpu.roll(done[p], c[1] % ny, axis=1)
                post[step, p, z + 1, pl.ds(x0 + 8, 8), :] = value

    copies = {}

    def copy(step, slot, src, dst, peer):
        made = pltpu.make_async_remote_copy(
            src_ref=src,
            dst_ref=dst,
            send_sem=send.at[step, slot],
            recv_sem=recv.at[step, slot],
            device_id=peer,
            device_id_type=MESH,
        )
        made.start()
        copies[step, slot] = [made, False]

    def arrive(step, slot):
        made = copies[step, slot]
        if not made[1]:
            made[1] = True
            made[0].wait_recv()
            return True
        return False

    def edge_slot(rising, side):
        return 2 + 2 * int(rising) + side

    def plane_slot(rising, part):
        return 6 + chunks * int(rising) + part

    def save_face(step, z, side):
        row = (7 + cx, 8)[side]
        for j, p in enumerate(FACES[side]):
            rows_out[step, side, z, j, :] = post[step, p, z + 1, row, :]

    def send_face(step, side):
        copy(
            step,
            side,
            rows_out.at[step, side],
            rows_in.at[step, side, pl.ds(1, cz)],
            (slab, (right, left)[side]),
        )

    def send_edge(step, rising, side):
        z, slot, peer = (top_z, 0, above) if rising else (0, cz + 1, below)
        copy(
            step,
            edge_slot(rising, side),
            rows_out.at[step, side, z],
            rows_in.at[step, side, slot],
            (peer, (right, left)[side]),
        )

    def send_plane(step, rising, part):
        z, slot, peer = (top_z, 0, above) if rising else (0, cz + 1, below)
        span = pl.ds(0 if rising else 5, 5)
        low, high = parts[part]
        here = pl.ds(8 + low, high - low)
        copy(
            step,
            plane_slot(rising, part),
            post.at[step, span, z + 1, here, :],
            post.at[step, span, slot, here, :],
            (peer, md),
        )

    def need(step, part, rising):
        for side in range(2):
            if part != outer[side]:
                continue
            row = (7, 8 + cx)[side]
            if arrive(step, side):
                for z in range(cz):
                    for j, p in enumerate(FACES[side]):
                        post[step, p, z + 1, row, :] = rows_in[step, side, z + 1, j, :]
            if arrive(step, edge_slot(not rising, side)):
                slot = cz + 1 if rising else 0
                sign = -1 if rising else 1
                for j, p in enumerate(FACES[side]):
                    if DIRS[p][2] == sign:
                        post[step, p, slot, row, :] = rows_in[step, side, slot, j, :]
        low, high = parts[part]
        for other in range(chunks):
            if parts[other][0] <= high and parts[other][1] >= low:
                arrive(step, plane_slot(not rising, other))

    def send_chunk(step, rising, part):
        z = top_z if rising else 0
        for side in range(2):
            if part == outer[1 - side]:
                save_face(step, z, side)
                send_edge(step, rising, side)
        send_plane(step, rising, part)

    def lattice_step(step):
        for part in range(chunks):
            if step == 0:
                f_parts[part].wait()
                if part == 0:
                    relax_part.wait()
            for rising in (True, False):
                if step:
                    with mark("need"):
                        need(step - 1, part, rising)
                with mark("collide"):
                    collide_chunk(step, top_z if rising else 0, part)
                if step or part:
                    send_chunk(step, rising, part)
            for z in range(1, top_z):
                collide_chunk(step, z, part)
                for side in range(2):
                    if part == outer[1 - side]:
                        save_face(step, z, side)
            if step == 0 and part == 0:
                with mark("barrier"):
                    pl.semaphore_wait(barrier, devices - 1)
                for rising in (True, False):
                    send_chunk(step, rising, part)
            for side in range(2):
                if part == outer[1 - side]:
                    send_face(step, side)

    def pair_forces():
        for g in range(groups):
            mine = [jnp.broadcast_to(at[c, pl.ds(g, 1), :], (8, 128)) for c in range(3)]
            sums = [jnp.zeros((8, 128), jnp.float32)] * 3
            for k in range(0, entries, 8):
                index = nbr_ref[pl.ds(k, 8), pl.ds(g * 128, 128)]
                lane, row = index & 127, index >> 7
                found = [None] * 3
                for h in range(groups):
                    pick = row == h
                    for c in range(3):
                        line = jnp.broadcast_to(at[c, pl.ds(h, 1), :], (8, 128))
                        value = lane_gather(line, lane)
                        found[c] = value if h == 0 else jnp.where(pick, value, found[c])
                gap = [found[c] - mine[c] for c in range(3)]
                weight = jnp.exp(-0.5 * (gap[0] * gap[0] + gap[1] * gap[1] + gap[2] * gap[2]))
                sums = [sums[c] + gap[c] * weight for c in range(3)]
            for c in range(3):
                pull[c, pl.ds(g, 1), :] = jnp.sum(sums[c], axis=0, keepdims=True)

    def prepare_particles():
        for part in pos_parts:
            part.wait()
        for g in range(groups):
            here = pl.ds(g * 128, 128)
            for c in range(3):
                at[c, pl.ds(g, 1), :] = pos_ref[pl.ds(c, 1), here]
                at[3 + c, pl.ds(g, 1), :] = vel_ref[pl.ds(c, 1), here]
        pair_forces()

    def prepare_hits():
        slots_part.wait()
        data[...] = jnp.ones(data.shape, jnp.float32)
        tgt[...] = jnp.zeros(tgt.shape, jnp.float32)
        table[...] = jnp.zeros(table.shape, jnp.float32)
        for g in range(groups):
            label = lax.broadcasted_iota(jnp.int32, (slot_count, 128), 0)
            same = label == slots_ref[pl.ds(g, 1), :]
            hits[:, pl.ds(g * 128, 128)] = jnp.where(same, 1.0, 0.0).astype(jnp.bfloat16)

    def prepare_routes():
        own_part.wait()
        top = own_ref.shape[1]
        owner = [
            jnp.concatenate([own_ref[z, pl.ds(k, 1), :] for z in range(cz)], axis=1)
            for k in range(top)
        ]
        label = lax.broadcasted_iota(jnp.int32, (devices, cells), 0)
        owned = [jnp.where(label == owner[k], 1.0, 0.0) for k in range(top)]
        earlier = lax.broadcasted_iota(jnp.int32, (cells, cells), 0) < lax.broadcasted_iota(
            jnp.int32, (cells, cells), 1
        )
        before = by_hits(
            total_of(owned), jnp.where(earlier, 1.0, 0.0).astype(jnp.bfloat16), ((1,), (0,))
        )
        start = (label * cap).astype(jnp.float32)
        place = lax.broadcasted_iota(jnp.int32, (slot_count, cells), 0).astype(jnp.float32)
        filled = jnp.zeros((slot_count, cells), jnp.float32)
        for k in range(top):
            spot = jnp.sum((before + start) * owned[k], axis=0, keepdims=True)
            filled = filled + jnp.where(place == spot, 1.0, 0.0)
            before = before + owned[k]
        placed[...] = filled.astype(jnp.bfloat16)

    def swap(turn, values, meanwhile):
        per = 128 // cap
        for d in range(devices):
            part = values[:, d // per * 128 : (d // per + 1) * 128]
            shift = (128 - d % per * cap) % 128
            blocks_out[turn, d] = part if shift == 0 else pltpu.roll(part, shift, axis=1)
        with mark("begin"):
            for k in sorted(range(1, devices), key=lambda k: -min(k // n_md, n_slab - k // n_md)):
                peer = peer_of(k)
                pltpu.make_async_remote_copy(
                    src_ref=blocks_out.at[turn, peer[0] * n_md + peer[1]],
                    dst_ref=blocks_in.at[turn, k],
                    send_sem=swap_send.at[turn],
                    recv_sem=swap_recv.at[turn],
                    device_id=peer,
                    device_id_type=MESH,
                ).start()
        blocks_in[turn, 0] = blocks_out[turn, me]
        meanwhile()
        everyone = pltpu.make_async_remote_copy(
            src_ref=blocks_out.at[turn, pl.ds(1, devices - 1)],
            dst_ref=blocks_in.at[turn, pl.ds(1, devices - 1)],
            send_sem=swap_send.at[turn],
            recv_sem=swap_recv.at[turn],
            device_id=(above, md),
            device_id_type=MESH,
        )
        with mark("landed"):
            everyone.wait_recv()
        zone = lax.broadcasted_iota(jnp.int32, (4, 128), 1) // cap
        lines = []
        for h in range(slot_count // 128):
            line = jnp.zeros((4, 128), jnp.float32)
            for j in range(per):
                source = h * per + j
                apart = wrapped(slab + n_slab - source // n_md, n_slab) * n_md + wrapped(
                    md + n_md - source % n_md, n_md
                )
                value = blocks_in[turn, apart]
                if j:
                    value = pltpu.roll(value, j * cap, axis=1)
                line = jnp.where(zone == j, value, line)
            lines.append(line)
        return lines, everyone.wait_send

    lattice_step(0)
    with mark("prep_part"):
        prepare_particles()
    lattice_step(1)
    with mark("hits"):
        prepare_hits()
    lattice_step(2)
    with mark("routes"):
        prepare_routes()
    for step in range(3, LB_STEPS):
        lattice_step(step)

    def finish_chunk(z, part):
        for x0 in range(*parts[part], 8):
            f = load(LB_STEPS, z, x0)
            for p in range(19):
                out_ref[ORDER[p], z, pl.ds(x0, 8), :] = f[p]
            density, vel = fields(f)
            for c, value in enumerate((*vel, density)):
                mean_ref[c, pl.ds(x0 + z * cx, 8), :] = value

    for part in range(chunks):
        for rising in (True, False):
            with mark("need_last"):
                need(LB_STEPS - 1, part, rising)
            finish_chunk(top_z if rising else 0, part)
        for z in range(1, top_z):
            finish_chunk(z, part)

    with mark("mean"):
        for c in range(4):
            scale = (velocity_scale if c < 3 else 1.0) / ny
            mean = jnp.sum(mean_ref[c].T, axis=0, keepdims=True) * scale
            for part, piece in enumerate(thirds(mean)):
                tgt[pl.ds(part * 4 + c, 1), :] = piece
        sums = by_hits(tgt[...], placed[...], ((1,), (1,)))

    def lattice_sent():
        for made, _ in copies.values():
            made.wait_send()

    with mark("swap0"):
        lines, sent_first = swap(0, sums[0:4] + sums[4:8] + sums[8:12], lattice_sent)

    slots = slots_ref[...]
    lane, row = slots & 127, slots >> 7
    goal = []
    for c in range(4):
        value = jnp.zeros((groups, 128), jnp.float32)
        for h, line in enumerate(lines):
            spread = jnp.broadcast_to(line[c : c + 1, :], (groups, 128))
            value = jnp.where(row == h, lane_gather(spread, lane), value)
        goal.append(value)
    rate = friction * goal[3]

    def advance():
        for c in range(3):
            vel = at[3 + c]
            force = pair_strength * pull[c] + rate * (goal[c] - vel)
            vel = vel + time_step * force
            at[3 + c] = vel
            at[c] = at[c] + time_step * vel

    def one_step(step, carry):
        with mark("pair"):
            pair_forces()
        with mark("advance"):
            advance()
        return carry

    advance()
    lax.fori_loop(1, MD_STEPS, one_step, 0)
    with mark("moments"):
        at[6] = at[3] * at[3] + at[4] * at[4] + at[5] * at[5]
        for c in range(4):
            for part, piece in enumerate(thirds(at[3 + c])):
                for g in range(groups):
                    data[pl.ds(part * 4 + c, 1), pl.ds(g * 128, 128)] = piece[g : g + 1, :]
        sums = by_hits(data[...], hits[...], ((1,), (1,)))
        moments = (sums[0:4] + sums[4:8] + sums[8:12]) / jnp.maximum(sums[12:13], 1.0)

    def put_particles():
        sent_first()
        for g in range(groups):
            here = pl.ds(g * 128, 128)
            for c in range(3):
                pos_out[pl.ds(c, 1), here] = at[c, pl.ds(g, 1), :]
                vel_out[pl.ds(c, 1), here] = at[3 + c, pl.ds(g, 1), :]

    with mark("swap1"):
        lines, sent_second = swap(1, moments, put_particles)
    for h, line in enumerate(lines):
        for part, piece in enumerate(thirds(line)):
            table[pl.ds(part * 4, 4), pl.ds(h * 128, 128)] = piece
    sums = by_hits(table[...], placed[...], ((1,), (0,)))
    picked = sums[0:4] + sums[4:8] + sums[8:12]
    for c in range(4):
        for z in range(cz):
            cell_out[c, pl.ds(z, 1), :] = picked[c : c + 1, z * cx : (z + 1) * cx]
    sent_second()


def on_device(populations, relax, owners, positions, velocities, neighbours, atom_slots):
    cz, cx, ny = relax.shape
    n_slab = lax.axis_size("slab")
    n_md = lax.axis_size("md")
    devices = n_slab * n_md
    top = owners.shape[2]
    cap = cz * max(2, 2 * cx * top // devices)
    slots = devices * cap
    atoms, entries = neighbours.shape
    groups = atoms // 128
    cells = cz * cx
    chunks = len(parts_of(cx))
    vmem = pl.BlockSpec(memory_space=pltpu.VMEM)
    hbm = pl.BlockSpec(memory_space=pltpu.HBM)
    dma = pltpu.SemaphoreType.DMA
    return pl.pallas_call(
        functools.partial(coupled_kernel, n_slab, n_md),
        out_shape=(
            jax.ShapeDtypeStruct(populations.shape, jnp.float32),
            jax.ShapeDtypeStruct(positions.shape, jnp.float32),
            jax.ShapeDtypeStruct(velocities.shape, jnp.float32),
            jax.ShapeDtypeStruct((4, cz, cx), jnp.float32),
        ),
        in_specs=[hbm] * 7,
        out_specs=(vmem,) * 4,
        scratch_shapes=[
            pltpu.VMEM(populations.shape, jnp.float32),
            pltpu.VMEM(relax.shape, jnp.float32),
            pltpu.VMEM((cz, top, cx), jnp.int32),
            pltpu.VMEM(positions.shape, jnp.float32),
            pltpu.VMEM(velocities.shape, jnp.float32),
            pltpu.VMEM((entries, atoms), jnp.int32),
            pltpu.VMEM((groups, 128), jnp.int32),
            dma((chunks + 6,)),
            pltpu.VMEM((LB_STEPS, 19, cz + 2, cx + 16, ny), jnp.float32),
            pltpu.VMEM((LB_STEPS, 2, cz, 8, ny), jnp.float32),
            pltpu.VMEM((LB_STEPS, 2, cz + 2, 8, ny), jnp.float32),
            pltpu.VMEM((4, cells, ny), jnp.float32),
            pltpu.VMEM((7, groups, 128), jnp.float32),
            pltpu.VMEM((3, groups, 128), jnp.float32),
            pltpu.VMEM((16, atoms), jnp.float32),
            pltpu.VMEM((slots, atoms), jnp.bfloat16),
            pltpu.VMEM((slots, cells), jnp.bfloat16),
            pltpu.VMEM((16, cells), jnp.float32),
            pltpu.VMEM((16, slots), jnp.float32),
            pltpu.VMEM((2, devices, 4, 128), jnp.float32),
            pltpu.VMEM((2, devices, 4, 128), jnp.float32),
            dma((LB_STEPS, 6 + 2 * chunks)),
            dma((LB_STEPS, 6 + 2 * chunks)),
            dma((2,)),
            dma((2,)),
        ],
        compiler_params=pltpu.CompilerParams(
            collective_id=0, has_side_effects=True, vmem_limit_bytes=67043328
        ),
        name="coupled",
    )(
        populations,
        relax,
        owners.transpose(0, 2, 1),
        positions,
        velocities,
        neighbours.T,
        atom_slots.reshape(groups, 128),
    )


def solution(mesh):
    return jax.shard_map(
        on_device,
        mesh=mesh,
        in_specs=(
            P(None, "slab", "md", None),
            P("slab", "md", None),
            P("slab", "md", None),
            P(None, ("slab", "md")),
            P(None, ("slab", "md")),
            P(("slab", "md"), None),
            P(("slab", "md")),
        ),
        out_specs=(
            P(None, "slab", "md", None),
            P(None, ("slab", "md")),
            P(None, ("slab", "md")),
            P(None, "slab", "md"),
        ),
        check_vma=False,
    )
```

time: 80.9 us -> 65.4 us (0.81)
  Pallas kernels: 71 us -> 60.2 us
  local copies, waits for them, and re-layouts: 8.81 us -> 4.29 us
    pallas_call x1, Pallas kernels: 71 us -> 60.2 us  [on_device(): pl.pallas_call(functools.partial(coupled_kernel, n_slab, n_md), out_shape...]
    unnamed x17 -> x10, local copies, waits for them, and re-layouts: 8.72 us -> 4.29 us
where the time goes in v1:
time: 65.4 us; the launch traced here: 65.2 us
  Pallas kernels  60.2 us (92%)
  local copies, waits for them, and re-layouts  4.29 us (7%)
  between operations  0.67 us (1%)
    pallas_call x1, Pallas kernels, on_device(): pl.pallas_call(functools.partial(coupled_kernel, n_slab, n_md), out_shape...  60.2 us
    unnamed x10, local copies, waits for them, and re-layouts  4.29 us

profile of v1, /device:TPU:0, one launch (start us, length us, event | category | flops | bytes accessed | tf_op | source)
XLA Modules:
  0.0 65.2 jit_solution(974952836487964543)
XLA Ops:
  0.6 60.2 %coupled.1 = (f32[19,2,64,128]{3,2,1,0:T(8,128)}, f32[3,1024]{1,0:T(4,128)}, f32[3,1024]{1,0:T(4,128)}, f32[4,2,64]{2,1,0:T(2,128)}) custom-call(f32[19,2,64,128]{3,2,1,0:T(8,128)} %f_hbm.1, f32[2,64,128]{2,1,0:T(8,128)} %relax_hbm.1, s32[2,2,64]{2,1,0:T(2,128)} %bitcast.5, f32[3,1024]{1,0:T(4,128)} %pos_hbm.1, f32[3,1024]{1,0:T(4,128)} %vel_hbm.1, ...), custom_call_target="tpu_custom_call" | custom-call | tf_op jit(solution)/shard_map/coupled/pallas_call | solution.py:572
  60.9 0.0 copy-start.1
  60.9 0.0 copy-start
  60.9 0.0 copy-start.2
  60.9 2.5 %copy.15 = f32[19,2,64,128]{3,2,1,0:T(8,128)} copy(f32[19,2,64,128]{3,2,1,0:T(8,128)} %get-tuple-element.8) | data formatting | bytes 2490368
  63.4 0.0 copy-done.1
  63.4 0.6 copy.16
  64.0 0.0 copy-done
  64.0 0.6 copy.17
  64.6 0.0 copy-done.2
  64.6 0.6 copy.18
Async XLA Ops:
  60.9 2.5 %copy-start.1 = (f32[3,1024]{1,0:T(4,128)S(1)}, f32[3,1024]{1,0:T(4,128)}, u32[]{:S(2)}) copy-start(f32[3,1024]{1,0:T(4,128)} %get-tuple-element.9) | copy-start | bytes 36868
  60.9 3.1 %copy-start = (f32[3,1024]{1,0:T(4,128)S(1)}, f32[3,1024]{1,0:T(4,128)}, u32[]{:S(2)}) copy-start(f32[3,1024]{1,0:T(4,128)} %get-tuple-element.10) | copy-start | bytes 36868
  60.9 3.7 %copy-start.2 = (f32[4,2,64]{2,1,0:T(2,128)S(1)}, f32[4,2,64]{2,1,0:T(2,128)}, u32[]{:S(2)}) copy-start(f32[4,2,64]{2,1,0:T(2,128)} %get-tuple-element.11) | copy-start | bytes 6148

commit v2 on v1

--- a/solution.py
+++ b/solution.py
@@ -147,6 +147,9 @@
     mean_ref,
     at,
     pull,
+    steps_at,
+    pairs_at,
+    span,
     data,
     hits,
     placed,
@@ -186,9 +189,6 @@
     def source_of(k):
         return wrapped(slab + n_slab - k // n_md, n_slab), wrapped(md + n_md - k % n_md, n_md)
 
-    for k in range(1, devices):
-        pl.semaphore_signal(barrier, inc=1, device_id=peer_of(k), device_id_type=MESH)
-
     loads = []
 
     def fetch(src, dst):
@@ -198,11 +198,19 @@
         return made
 
     f_parts = []
-    for low, high in parts:
-        here = pl.ds(low, high - low)
-        f_parts.append(fetch(f_hbm.at[:, :, here, :], f_ref.at[:, :, here, :]))
+    for low, high in parts[:2] + [(8, cx - 8)]:
+        if low < high:
+            here = pl.ds(low, high - low)
+            f_parts.append(fetch(f_hbm.at[:, :, here, :], f_ref.at[:, :, here, :]))
         if len(f_parts) == 1:
             relax_part = fetch(relax_hbm, relax_ref)
+    if max(n_slab // 2, n_md // 2) <= LB_STEPS:
+        near = {(a % n_slab) * n_md + b % n_md for a in (-1, 0, 1) for b in (-1, 0, 1)}
+        greeted = sorted(near - {0})
+    else:
+        greeted = list(range(1, devices))
+    for k in greeted:
+        pl.semaphore_signal(barrier, inc=1, device_id=peer_of(k), device_id_type=MESH)
     pos_parts = [fetch(pos_hbm, pos_ref), fetch(vel_hbm, vel_ref), fetch(nbr_hbm, nbr_ref)]
     slots_part = fetch(slots_hbm, slots_ref)
     own_part = fetch(own_hbm, own_ref)
@@ -222,33 +230,34 @@
                 value = done[p] if c[1] == 0 else pltpu.roll(done[p], c[1] % ny, axis=1)
                 post[step, p, z + 1, pl.ds(x0 + 8, 8), :] = value
 
-    copies = {}
-
-    def copy(step, slot, src, dst, peer):
-        made = pltpu.make_async_remote_copy(
+    def copy(step, kind, slot, src, dst, peer):
+        pltpu.make_async_remote_copy(
             src_ref=src,
             dst_ref=dst,
-            send_sem=send.at[step, slot],
-            recv_sem=recv.at[step, slot],
+            send_sem=send.at[kind],
+            recv_sem=recv.at[step % 2, slot],
             device_id=peer,
             device_id_type=MESH,
+        ).start()
+
+    def whole(src, dst, send_sem, recv_sem):
+        return pltpu.make_async_remote_copy(
+            src_ref=src,
+            dst_ref=dst,
+            send_sem=send_sem,
+            recv_sem=recv_sem,
+            device_id=(above, md),
+            device_id_type=MESH,
         )
-        made.start()
-        copies[step, slot] = [made, False]
-
-    def arrive(step, slot):
-        made = copies[step, slot]
-        if not made[1]:
-            made[1] = True
-            made[0].wait_recv()
-            return True
-        return False
-
-    def edge_slot(rising, side):
-        return 2 + 2 * int(rising) + side
-
-    def plane_slot(rising, part):
-        return 6 + chunks * int(rising) + part
+
+    arrived = set()
+
+    def arrive(step, slot, ref):
+        if (step, slot) in arrived:
+            return False
+        arrived.add((step, slot))
+        whole(ref, ref, send.at[0], recv.at[step % 2, slot]).wait_recv()
+        return True
 
     def save_face(step, z, side):
         row = (7 + cx, 8)[side]
@@ -258,6 +267,7 @@
     def send_face(step, side):
         copy(
             step,
+            0,
             side,
             rows_out.at[step, side],
             rows_in.at[step, side, pl.ds(1, cz)],
@@ -268,7 +278,8 @@
         z, slot, peer = (top_z, 0, above) if rising else (0, cz + 1, below)
         copy(
             step,
-            edge_slot(rising, side),
+            1,
+            side,
             rows_out.at[step, side, z],
             rows_in.at[step, side, slot],
             (peer, (right, left)[side]),
@@ -281,31 +292,29 @@
         here = pl.ds(8 + low, high - low)
         copy(
             step,
-            plane_slot(rising, part),
+            2,
+            2 + part,
             post.at[step, span, z + 1, here, :],
             post.at[step, span, slot, here, :],
             (peer, md),
         )
 
-    def need(step, part, rising):
+    def need(step, part):
         for side in range(2):
-            if part != outer[side]:
+            if part != outer[side] or not arrive(step, side, rows_in.at[step, side]):
                 continue
             row = (7, 8 + cx)[side]
-            if arrive(step, side):
+            for j, p in enumerate(FACES[side]):
                 for z in range(cz):
-                    for j, p in enumerate(FACES[side]):
-                        post[step, p, z + 1, row, :] = rows_in[step, side, z + 1, j, :]
-            if arrive(step, edge_slot(not rising, side)):
-                slot = cz + 1 if rising else 0
-                sign = -1 if rising else 1
-                for j, p in enumerate(FACES[side]):
-                    if DIRS[p][2] == sign:
-                        post[step, p, slot, row, :] = rows_in[step, side, slot, j, :]
+                    post[step, p, z + 1, row, :] = rows_in[step, side, z + 1, j, :]
+                if DIRS[p][2]:
+                    slot = 0 if DIRS[p][2] == 1 else cz + 1
+                    post[step, p, slot, row, :] = rows_in[step, side, slot, j, :]
         low, high = parts[part]
-        for other in range(chunks):
-            if parts[other][0] <= high and parts[other][1] >= low:
-                arrive(step, plane_slot(not rising, other))
+        for other, (first, last) in enumerate(parts):
+            if first <= high and last >= low:
+                here = pl.ds(8 + first, last - first)
+                arrive(step, 2 + other, post.at[step, pl.ds(0, 10), 0, here, :])
 
     def send_chunk(step, rising, part):
         z = top_z if rising else 0
@@ -318,13 +327,14 @@
     def lattice_step(step):
         for part in range(chunks):
             if step == 0:
-                f_parts[part].wait()
+                if part < len(f_parts):
+                    f_parts[part].wait()
                 if part == 0:
                     relax_part.wait()
+            if step:
+                with mark("need"):
+                    need(step - 1, part)
             for rising in (True, False):
-                if step:
-                    with mark("need"):
-                        need(step - 1, part, rising)
                 with mark("collide"):
                     collide_chunk(step, top_z if rising else 0, part)
                 if step or part:
@@ -336,7 +346,7 @@
                         save_face(step, z, side)
             if step == 0 and part == 0:
                 with mark("barrier"):
-                    pl.semaphore_wait(barrier, devices - 1)
+                    pl.semaphore_wait(barrier, len(greeted))
                 for rising in (True, False):
                     send_chunk(step, rising, part)
             for side in range(2):
@@ -363,6 +373,70 @@
             for c in range(3):
                 pull[c, pl.ds(g, 1), :] = jnp.sum(sums[c], axis=0, keepdims=True)
 
+    half = groups // 2
+    levels = 65535.0
+    most_pull = 0.6066
+
+    def extreme(value, pick):
+        return jnp.broadcast_to(pick(pick(value, axis=0, keepdims=True), axis=1, keepdims=True), (1, 128))
+
+    def prepare_span():
+        places = jnp.concatenate([at[c] for c in range(3)], axis=0)
+        speeds = jnp.concatenate([at[3 + c] for c in range(3)], axis=0)
+        span[pl.ds(0, 1), :] = extreme(places, jnp.min)
+        span[pl.ds(1, 1), :] = extreme(places, jnp.max)
+        span[pl.ds(2, 1), :] = extreme(jnp.abs(speeds), jnp.max)
+
+    def bound_span(goal, rate):
+        far = extreme(jnp.maximum(jnp.maximum(jnp.abs(goal[0]), jnp.abs(goal[1])), jnp.abs(goal[2])), jnp.max)
+        least, most = extreme(rate, jnp.min), extreme(rate, jnp.max)
+        tame = (least >= 0.0) & (time_step * most <= 1.0)
+        strong = time_step * jnp.maximum(jnp.abs(least), jnp.abs(most))
+        low, high, speed = (span[pl.ds(i, 1), :] for i in range(3))
+        for step in range(1, MD_STEPS):
+            speed = jnp.where(tame, jnp.maximum(speed, far), speed + strong * (speed + far))
+            speed = (speed + time_step * pair_strength * entries * most_pull) * 1.0001
+            low, high = low - time_step * speed, high + time_step * speed
+            width = jnp.maximum(high - low, 1e-20)
+            span[pl.ds(4 + 2 * step, 1), :] = low
+            span[pl.ds(5 + 2 * step, 1), :] = width * (1.0 / levels)
+
+    def coarse_forces(step):
+        low = span[pl.ds(4 + 2 * step, 1), :]
+        unit = span[pl.ds(5 + 2 * step, 1), :]
+        per_unit = 1.0 / unit
+        for c in range(3):
+            level = jnp.clip((at[c] - low) * per_unit + 0.5, 0.0, levels).astype(jnp.int32)
+            steps_at[c] = level
+            pairs_at[c] = level[:half] | (level[half:] << 16)
+        decay = (-0.5 * 1.4426950408889634) * (unit * unit)
+        for g in range(groups):
+            mine = [
+                jnp.broadcast_to(steps_at[c, pl.ds(g, 1), :].astype(jnp.float32), (8, 128)) for c in range(3)
+            ]
+            sums = [jnp.zeros((8, 128), jnp.float32)] * 3
+            for k in range(0, entries, 8):
+                index = nbr_ref[pl.ds(k, 8), pl.ds(g * 128, 128)]
+                lane, row = index & 127, index >> 7
+                upper = row >= half
+                row = jnp.where(upper, row - half, row)
+                shift = jnp.where(upper, 16, 0)
+                found = [None] * 3
+                for h in range(half):
+                    pick = row == h
+                    for c in range(3):
+                        line = jnp.broadcast_to(pairs_at[c, pl.ds(h, 1), :], (8, 128))
+                        value = lane_gather(line, lane)
+                        found[c] = value if h == 0 else jnp.where(pick, value, found[c])
+                gap = [
+                    (lax.shift_right_logical(found[c], shift) & 65535).astype(jnp.float32) - mine[c]
+                    for c in range(3)
+                ]
+                weight = jnp.exp2((gap[0] * gap[0] + gap[1] * gap[1] + gap[2] * gap[2]) * decay)
+                sums = [sums[c] + gap[c] * weight for c in range(3)]
+            for c in range(3):
+                pull[c, pl.ds(g, 1), :] = jnp.sum(sums[c], axis=0, keepdims=True) * unit
+
     def prepare_particles():
         for part in pos_parts:
             part.wait()
@@ -371,6 +445,7 @@
             for c in range(3):
                 at[c, pl.ds(g, 1), :] = pos_ref[pl.ds(c, 1), here]
                 at[3 + c, pl.ds(g, 1), :] = vel_ref[pl.ds(c, 1), here]
+        prepare_span()
         pair_forces()
 
     def prepare_hits():
@@ -409,47 +484,55 @@
 
     def swap(turn, values, meanwhile):
         per = 128 // cap
-        for d in range(devices):
-            part = values[:, d // per * 128 : (d // per + 1) * 128]
-            shift = (128 - d % per * cap) % 128
-            blocks_out[turn, d] = part if shift == 0 else pltpu.roll(part, shift, axis=1)
+        zone = lax.broadcasted_iota(jnp.int32, (4, 128), 1) // cap
+        step = lax.broadcasted_iota(jnp.int32, (4, 128), 0)
+        for h in range(slot_count // 128):
+            turned = pltpu.roll(
+                values[:, h * 128 : (h + 1) * 128], 0, axis=1, stride=cap, stride_axis=0
+            )
+            for j in range(per):
+                own = zone == (step + j) % per
+                blocks_out[turn, h * per + j] = jnp.sum(
+                    jnp.where(own, turned, 0.0), axis=0, keepdims=True
+                )
         with mark("begin"):
             for k in sorted(range(1, devices), key=lambda k: -min(k // n_md, n_slab - k // n_md)):
                 peer = peer_of(k)
                 pltpu.make_async_remote_copy(
                     src_ref=blocks_out.at[turn, peer[0] * n_md + peer[1]],
-                    dst_ref=blocks_in.at[turn, k],
+                    dst_ref=blocks_in.at[turn, me],
                     send_sem=swap_send.at[turn],
                     recv_sem=swap_recv.at[turn],
                     device_id=peer,
                     device_id_type=MESH,
                 ).start()
-        blocks_in[turn, 0] = blocks_out[turn, me]
+        blocks_in[turn, me] = blocks_out[turn, me]
         meanwhile()
-        everyone = pltpu.make_async_remote_copy(
-            src_ref=blocks_out.at[turn, pl.ds(1, devices - 1)],
-            dst_ref=blocks_in.at[turn, pl.ds(1, devices - 1)],
-            send_sem=swap_send.at[turn],
-            recv_sem=swap_recv.at[turn],
-            device_id=(above, md),
-            device_id_type=MESH,
+        others = pl.ds(1, devices - 1)
+        everyone = whole(
+            blocks_out.at[turn, others],
+            blocks_in.at[turn, others],
+            swap_send.at[turn],
+            swap_recv.at[turn],
         )
         with mark("landed"):
             everyone.wait_recv()
-        zone = lax.broadcasted_iota(jnp.int32, (4, 128), 1) // cap
+        back = 128 - (me % per) * cap
+        zone = lax.broadcasted_iota(jnp.int32, (8, 128), 1) // cap
+        step = lax.broadcasted_iota(jnp.int32, (8, 128), 0)
         lines = []
         for h in range(slot_count // 128):
-            line = jnp.zeros((4, 128), jnp.float32)
-            for j in range(per):
-                source = h * per + j
-                apart = wrapped(slab + n_slab - source // n_md, n_slab) * n_md + wrapped(
-                    md + n_md - source % n_md, n_md
-                )
-                value = blocks_in[turn, apart]
-                if j:
-                    value = pltpu.roll(value, j * cap, axis=1)
-                line = jnp.where(zone == j, value, line)
-            lines.append(line)
+            rows = [jnp.zeros((1, 128), jnp.float32)] * 4
+            for b in range(per // 8):
+                block = pltpu.roll(blocks_in[turn, pl.ds(h * per + b * 8, 8), 0, :], back, axis=1)
+                turned = pltpu.roll(block, 0, axis=1, stride=cap, stride_axis=0)
+                for c in range(4):
+                    row = jnp.sum(
+                        jnp.where(zone == (step + c) % per, turned, 0.0), axis=0, keepdims=True
+                    )
+                    shift = (b * 8 - c) * cap % 128
+                    rows[c] = rows[c] + (row if shift == 0 else pltpu.roll(row, shift, axis=1))
+            lines.append(jnp.concatenate(rows, axis=0))
         return lines, everyone.wait_send
 
     lattice_step(0)
@@ -474,9 +557,9 @@
                 mean_ref[c, pl.ds(x0 + z * cx, 8), :] = value
 
     for part in range(chunks):
+        with mark("need_last"):
+            need(LB_STEPS - 1, part)
         for rising in (True, False):
-            with mark("need_last"):
-                need(LB_STEPS - 1, part, rising)
             finish_chunk(top_z if rising else 0, part)
         for z in range(1, top_z):
             finish_chunk(z, part)
@@ -490,8 +573,9 @@
         sums = by_hits(tgt[...], placed[...], ((1,), (1,)))
 
     def lattice_sent():
-        for made, _ in copies.values():
-            made.wait_send()
+        planes = post.at[:, pl.ds(0, 10), 0, pl.ds(8, cx), :]
+        for kind, ref in enumerate((rows_out, rows_out.at[:, :, pl.ds(0, 2)], planes)):
+            whole(ref, ref, send.at[kind], recv.at[0, 0]).wait_send()
 
     with mark("swap0"):
         lines, sent_first = swap(0, sums[0:4] + sums[4:8] + sums[8:12], lattice_sent)
@@ -517,11 +601,12 @@
 
     def one_step(step, carry):
         with mark("pair"):
-            pair_forces()
+            coarse_forces(step)
         with mark("advance"):
             advance()
         return carry
 
+    bound_span(goal, rate)
     advance()
     lax.fori_loop(1, MD_STEPS, one_step, 0)
     with mark("moments"):
@@ -552,6 +637,17 @@
         for z in range(cz):
             cell_out[c, pl.ds(z, 1), :] = picked[c : c + 1, z * cx : (z + 1) * cx]
     sent_second()
+
+
+def put_out(*refs):
+    count = len(refs) // 2
+    copies = [
+        pltpu.make_async_copy(refs[i], refs[count + i], refs[-1].at[i]) for i in range(count)
+    ]
+    for made in copies:
+        made.start()
+    for made in copies:
+        made.wait()
 
 
 def on_device(populations, relax, owners, positions, velocities, neighbours, atom_slots):
@@ -569,14 +665,19 @@
     vmem = pl.BlockSpec(memory_space=pltpu.VMEM)
     hbm = pl.BlockSpec(memory_space=pltpu.HBM)
     dma = pltpu.SemaphoreType.DMA
-    return pl.pallas_call(
+    held = [populations.shape, positions.shape, velocities.shape, (4, cz, cx)]
+    args = (
+        populations,
+        relax,
+        owners.transpose(0, 2, 1),
+        positions,
+        velocities,
+        neighbours.T,
+        atom_slots.reshape(groups, 128),
+    )
+    results = pl.pallas_call(
         functools.partial(coupled_kernel, n_slab, n_md),
-        out_shape=(
-            jax.ShapeDtypeStruct(populations.shape, jnp.float32),
-            jax.ShapeDtypeStruct(positions.shape, jnp.float32),
-            jax.ShapeDtypeStruct(velocities.shape, jnp.float32),
-            jax.ShapeDtypeStruct((4, cz, cx), jnp.float32),
-        ),
+        out_shape=tuple(pltpu.VMEM(shape, jnp.float32) for shape in held),
         in_specs=[hbm] * 7,
         out_specs=(vmem,) * 4,
         scratch_shapes=[
@@ -587,38 +688,42 @@
             pltpu.VMEM(velocities.shape, jnp.float32),
             pltpu.VMEM((entries, atoms), jnp.int32),
             pltpu.VMEM((groups, 128), jnp.int32),
-            dma((chunks + 6,)),
+            dma((9,)),
             pltpu.VMEM((LB_STEPS, 19, cz + 2, cx + 16, ny), jnp.float32),
             pltpu.VMEM((LB_STEPS, 2, cz, 8, ny), jnp.float32),
             pltpu.VMEM((LB_STEPS, 2, cz + 2, 8, ny), jnp.float32),
             pltpu.VMEM((4, cells, ny), jnp.float32),
             pltpu.VMEM((7, groups, 128), jnp.float32),
             pltpu.VMEM((3, groups, 128), jnp.float32),
+            pltpu.VMEM((3, groups, 128), jnp.int32),
+            pltpu.VMEM((3, groups // 2, 128), jnp.int32),
+            pltpu.VMEM((4 + 2 * MD_STEPS, 128), jnp.float32),
             pltpu.VMEM((16, atoms), jnp.float32),
             pltpu.VMEM((slots, atoms), jnp.bfloat16),
             pltpu.VMEM((slots, cells), jnp.bfloat16),
             pltpu.VMEM((16, cells), jnp.float32),
             pltpu.VMEM((16, slots), jnp.float32),
-            pltpu.VMEM((2, devices, 4, 128), jnp.float32),
-            pltpu.VMEM((2, devices, 4, 128), jnp.float32),
-            dma((LB_STEPS, 6 + 2 * chunks)),
-            dma((LB_STEPS, 6 + 2 * chunks)),
+            pltpu.VMEM((2, devices, 1, 128), jnp.float32),
+            pltpu.VMEM((2, devices, 1, 128), jnp.float32),
+            dma((3,)),
+            dma((2, 2 + chunks)),
             dma((2,)),
             dma((2,)),
         ],
         compiler_params=pltpu.CompilerParams(
-            collective_id=0, has_side_effects=True, vmem_limit_bytes=67043328
+            collective_id=0, has_side_effects=True, vmem_limit_bytes=48 * 1024 * 1024
         ),
         name="coupled",
-    )(
-        populations,
-        relax,
-        owners.transpose(0, 2, 1),
-        positions,
-        velocities,
-        neighbours.T,
-        atom_slots.reshape(groups, 128),
-    )
+    )(*(pltpu.with_memory_space_constraint(arg, pltpu.HBM) for arg in args))
+    return pl.pallas_call(
+        put_out,
+        out_shape=tuple(jax.ShapeDtypeStruct(shape, jnp.float32) for shape in held),
+        in_specs=[vmem] * 4,
+        out_specs=(hbm,) * 4,
+        scratch_shapes=[dma((4,))],
+        compiler_params=pltpu.CompilerParams(vmem_limit_bytes=4 * 1024 * 1024),
+        name="put_out",
+    )(*(pltpu.with_memory_space_constraint(part, pltpu.VMEM) for part in results))
 
 
 def solution(mesh):

time: 65.4 us -> 54.5 us (0.83)
  Pallas kernels: 60.2 us -> 53.7 us
  local copies, waits for them, and re-layouts: 4.29 us -> 0 us
    pallas_call x1, Pallas kernels: 60.2 us -> 52.6 us  [on_device(): pl.pallas_call(functools.partial(coupled_kernel, n_slab, n_md), out_shape...]
    unnamed x10 -> x0, local copies, waits for them, and re-layouts: 4.29 us -> none
    pallas_call x0 -> x1, Pallas kernels: none -> 1.08 us  [on_device(): pl.pallas_call(put_out, out_shape=tuple((jax.ShapeDtypeStruct(shape, jnp....]
where the time goes in v2:
time: 54.5 us; the launch traced here: 54.3 us
  Pallas kernels  53.7 us (99%)
  between operations  0.64 us (1%)
    pallas_call x1, Pallas kernels, on_device(): pl.pallas_call(functools.partial(coupled_kernel, n_slab, n_md), out_shape...  52.6 us

profile of v2, /device:TPU:0, one launch (start us, length us, event | category | flops | bytes accessed | tf_op | source)
XLA Modules:
  0.0 54.3 jit_solution(17829214256067600874)
XLA Ops:
  0.6 52.6 %coupled.1 = (f32[19,2,64,128]{3,2,1,0:T(8,128)S(1)}, f32[3,1024]{1,0:T(4,128)S(1)}, f32[3,1024]{1,0:T(4,128)S(1)}, f32[4,2,64]{2,1,0:T(2,128)S(1)}) custom-call(f32[19,2,64,128]{3,2,1,0:T(8,128)} %f_hbm.1, f32[2,64,128]{2,1,0:T(8,128)} %relax_hbm.1, s32[2,2,64]{2,1,0:T(2,128)} %bitcast.5, f32[3,1024]{1,0:T(4,128)} %pos_hbm.1, f32[3,1024]{1,0:T(4,128)} %vel_hbm.1, ...), custom_call_target="tpu_custom_call" | custom-call | tf_op jit(solution)/shard_map/coupled/pallas_call | solution.py:678
  53.2 1.1 %put_out.1 = (f32[19,2,64,128]{3,2,1,0:T(8,128)}, f32[3,1024]{1,0:T(4,128)}, f32[3,1024]{1,0:T(4,128)}, f32[4,2,64]{2,1,0:T(2,128)}) custom-call(f32[19,2,64,128]{3,2,1,0:T(8,128)S(1)} %get-tuple-element.8.refs_0_, f32[3,1024]{1,0:T(4,128)S(1)} %get-tuple-element.9.refs_1_, f32[3,1024]{1,0:T(4,128)S(1)} %get-tuple-element.10.refs_2_, ...), custom_call_target="tpu_custom_call" | custom-call | tf_op jit(solution)/shard_map/put_out/pallas_call | solution.py:718

commit v3 on v2

--- a/solution.py
+++ b/solution.py
@@ -144,6 +144,8 @@
     post,
     rows_out,
     rows_in,
+    edge_out,
+    edge_in,
     mean_ref,
     at,
     pull,
@@ -270,18 +272,22 @@
             0,
             side,
             rows_out.at[step, side],
-            rows_in.at[step, side, pl.ds(1, cz)],
+            rows_in.at[step, side],
             (slab, (right, left)[side]),
         )
 
+    EDGES = [[DIRS.index((x, 0, z)) for z in (-1, 1)] for x in (1, -1)]
+
     def send_edge(step, rising, side):
-        z, slot, peer = (top_z, 0, above) if rising else (0, cz + 1, below)
+        z, peer = (top_z, above) if rising else (0, below)
+        row = (7 + cx, 8)[side]
+        edge_out[step, side, int(rising), 0, :] = post[step, EDGES[side][int(rising)], z + 1, row, :]
         copy(
             step,
             1,
-            side,
-            rows_out.at[step, side, z],
-            rows_in.at[step, side, slot],
+            2 + side,
+            edge_out.at[step, side, int(rising)],
+            edge_in.at[step, side, int(rising)],
             (peer, (right, left)[side]),
         )
 
@@ -293,7 +299,7 @@
         copy(
             step,
             2,
-            2 + part,
+            4 + part,
             post.at[step, span, z + 1, here, :],
             post.at[step, span, slot, here, :],
             (peer, md),
@@ -306,15 +312,16 @@
             row = (7, 8 + cx)[side]
             for j, p in enumerate(FACES[side]):
                 for z in range(cz):
-                    post[step, p, z + 1, row, :] = rows_in[step, side, z + 1, j, :]
-                if DIRS[p][2]:
-                    slot = 0 if DIRS[p][2] == 1 else cz + 1
-                    post[step, p, slot, row, :] = rows_in[step, side, slot, j, :]
+                    post[step, p, z + 1, row, :] = rows_in[step, side, z, j, :]
+            arrive(step, 2 + side, edge_in.at[step, side])
+            for rising in range(2):
+                slot = 0 if rising else cz + 1
+                post[step, EDGES[side][rising], slot, row, :] = edge_in[step, side, rising, 0, :]
         low, high = parts[part]
         for other, (first, last) in enumerate(parts):
             if first <= high and last >= low:
                 here = pl.ds(8 + first, last - first)
-                arrive(step, 2 + other, post.at[step, pl.ds(0, 10), 0, here, :])
+                arrive(step, 4 + other, post.at[step, pl.ds(0, 10), 0, here, :])
 
     def send_chunk(step, rising, part):
         z = top_z if rising else 0
@@ -387,9 +394,18 @@
         span[pl.ds(1, 1), :] = extreme(places, jnp.max)
         span[pl.ds(2, 1), :] = extreme(jnp.abs(speeds), jnp.max)
 
-    def bound_span(goal, rate):
-        far = extreme(jnp.maximum(jnp.maximum(jnp.abs(goal[0]), jnp.abs(goal[1])), jnp.abs(goal[2])), jnp.max)
-        least, most = extreme(rate, jnp.min), extreme(rate, jnp.max)
+    def bound_span(blocks):
+        per = 128 // cap
+        zone = lax.broadcasted_iota(jnp.int32, (8, 128), 1) // cap
+        last = zone == lax.rem(lax.rem(me, per) + 3, per)
+        largest = smallest = None
+        strength = jnp.zeros((8, 128), jnp.float32)
+        for block in blocks:
+            strength = jnp.maximum(strength, jnp.where(last, 0.0, jnp.abs(block)))
+            rate = jnp.where(last, friction * block, 0.0)
+            largest = rate if largest is None else jnp.maximum(largest, rate)
+            smallest = rate if smallest is None else jnp.minimum(smallest, rate)
+        far, least, most = extreme(strength, jnp.max), extreme(smallest, jnp.min), extreme(largest, jnp.max)
         tame = (least >= 0.0) & (time_step * most <= 1.0)
         strong = time_step * jnp.maximum(jnp.abs(least), jnp.abs(most))
         low, high, speed = (span[pl.ds(i, 1), :] for i in range(3))
@@ -517,23 +533,23 @@
         )
         with mark("landed"):
             everyone.wait_recv()
-        back = 128 - (me % per) * cap
+        place = lax.rem(me, per)
         zone = lax.broadcasted_iota(jnp.int32, (8, 128), 1) // cap
         step = lax.broadcasted_iota(jnp.int32, (8, 128), 0)
-        lines = []
+        lines, blocks = [], []
         for h in range(slot_count // 128):
             rows = [jnp.zeros((1, 128), jnp.float32)] * 4
             for b in range(per // 8):
-                block = pltpu.roll(blocks_in[turn, pl.ds(h * per + b * 8, 8), 0, :], back, axis=1)
+                block = blocks_in[turn, pl.ds(h * per + b * 8, 8), 0, :]
+                blocks.append(block)
                 turned = pltpu.roll(block, 0, axis=1, stride=cap, stride_axis=0)
                 for c in range(4):
-                    row = jnp.sum(
-                        jnp.where(zone == (step + c) % per, turned, 0.0), axis=0, keepdims=True
-                    )
-                    shift = (b * 8 - c) * cap % 128
+                    own = zone == lax.rem(step + (c + place), per)
+                    row = jnp.sum(jnp.where(own, turned, 0.0), axis=0, keepdims=True)
+                    shift = b * 8 * cap
                     rows[c] = rows[c] + (row if shift == 0 else pltpu.roll(row, shift, axis=1))
-            lines.append(jnp.concatenate(rows, axis=0))
-        return lines, everyone.wait_send
+            lines.append(rows)
+        return lines, blocks, everyone.wait_send
 
     lattice_step(0)
     with mark("prep_part"):
@@ -574,19 +590,21 @@
 
     def lattice_sent():
         planes = post.at[:, pl.ds(0, 10), 0, pl.ds(8, cx), :]
-        for kind, ref in enumerate((rows_out, rows_out.at[:, :, pl.ds(0, 2)], planes)):
+        for kind, ref in enumerate((rows_out, edge_out, planes)):
             whole(ref, ref, send.at[kind], recv.at[0, 0]).wait_send()
 
     with mark("swap0"):
-        lines, sent_first = swap(0, sums[0:4] + sums[4:8] + sums[8:12], lattice_sent)
-
+        lines, blocks, sent_first = swap(0, sums[0:4] + sums[4:8] + sums[8:12], lattice_sent)
+
+    per = 128 // cap
     slots = slots_ref[...]
-    lane, row = slots & 127, slots >> 7
+    row = slots >> 7
     goal = []
     for c in range(4):
+        lane = (slots + (c + lax.rem(me, per)) * cap) & 127
         value = jnp.zeros((groups, 128), jnp.float32)
         for h, line in enumerate(lines):
-            spread = jnp.broadcast_to(line[c : c + 1, :], (groups, 128))
+            spread = jnp.broadcast_to(line[c], (groups, 128))
             value = jnp.where(row == h, lane_gather(spread, lane), value)
         goal.append(value)
     rate = friction * goal[3]
@@ -606,7 +624,7 @@
             advance()
         return carry
 
-    bound_span(goal, rate)
+    bound_span(blocks)
     advance()
     lax.fori_loop(1, MD_STEPS, one_step, 0)
     with mark("moments"):
@@ -627,10 +645,12 @@
                 vel_out[pl.ds(c, 1), here] = at[3 + c, pl.ds(g, 1), :]
 
     with mark("swap1"):
-        lines, sent_second = swap(1, moments, put_particles)
+        lines, _, sent_second = swap(1, moments, put_particles)
     for h, line in enumerate(lines):
-        for part, piece in enumerate(thirds(line)):
-            table[pl.ds(part * 4, 4), pl.ds(h * 128, 128)] = piece
+        for c in range(4):
+            whole_line = pltpu.roll(line[c], 128 - lax.rem(c + lax.rem(me, per), per) * cap, axis=1)
+            for part, piece in enumerate(thirds(whole_line)):
+                table[pl.ds(part * 4 + c, 1), pl.ds(h * 128, 128)] = piece
     sums = by_hits(table[...], placed[...], ((1,), (0,)))
     picked = sums[0:4] + sums[4:8] + sums[8:12]
     for c in range(4):
@@ -691,7 +711,9 @@
             dma((9,)),
             pltpu.VMEM((LB_STEPS, 19, cz + 2, cx + 16, ny), jnp.float32),
             pltpu.VMEM((LB_STEPS, 2, cz, 8, ny), jnp.float32),
-            pltpu.VMEM((LB_STEPS, 2, cz + 2, 8, ny), jnp.float32),
+            pltpu.VMEM((LB_STEPS, 2, cz, 8, ny), jnp.float32),
+            pltpu.VMEM((LB_STEPS, 2, 2, 1, ny), jnp.float32),
+            pltpu.VMEM((LB_STEPS, 2, 2, 1, ny), jnp.float32),
             pltpu.VMEM((4, cells, ny), jnp.float32),
             pltpu.VMEM((7, groups, 128), jnp.float32),
             pltpu.VMEM((3, groups, 128), jnp.float32),
@@ -706,7 +728,7 @@
             pltpu.VMEM((2, devices, 1, 128), jnp.float32),
             pltpu.VMEM((2, devices, 1, 128), jnp.float32),
             dma((3,)),
-            dma((2, 2 + chunks)),
+            dma((2, 4 + chunks)),
             dma((2,)),
             dma((2,)),
         ],

time: 54.5 us -> 52.7 us (0.967)
  Pallas kernels: 53.7 us -> 51.9 us
    pallas_call x1, Pallas kernels: 52.6 us -> 50.9 us  [on_device(): pl.pallas_call(functools.partial(coupled_kernel, n_slab, n_md), out_shape...]
where the time goes in v3:
time: 52.7 us; the launch traced here: 52.6 us
  Pallas kernels  51.9 us (98%)
  between operations  0.64 us (1%)
    pallas_call x1, Pallas kernels, on_device(): pl.pallas_call(functools.partial(coupled_kernel, n_slab, n_md), out_shape...  50.9 us
    pallas_call x1, Pallas kernels, on_device(): pl.pallas_call(put_out, out_shape=tuple((jax.ShapeDtypeStruct(shape, jnp....  1.08 us

profile of v3, /device:TPU:0, one launch (start us, length us, event | category | flops | bytes accessed | tf_op | source)
XLA Modules:
  0.0 52.6 jit_solution(16374803354133384082)
XLA Ops:
  0.6 50.9 %coupled.1 = (f32[19,2,64,128]{3,2,1,0:T(8,128)S(1)}, f32[3,1024]{1,0:T(4,128)S(1)}, f32[3,1024]{1,0:T(4,128)S(1)}, f32[4,2,64]{2,1,0:T(2,128)S(1)}) custom-call(f32[19,2,64,128]{3,2,1,0:T(8,128)} %f_hbm.1, f32[2,64,128]{2,1,0:T(8,128)} %relax_hbm.1, s32[2,2,64]{2,1,0:T(2,128)} %bitcast.5, f32[3,1024]{1,0:T(4,128)} %pos_hbm.1, f32[3,1024]{1,0:T(4,128)} %vel_hbm.1, ...), custom_call_target="tpu_custom_call" | custom-call | tf_op jit(solution)/shard_map/coupled/pallas_call | solution.py:698
  51.5 1.1 %put_out.1 = (f32[19,2,64,128]{3,2,1,0:T(8,128)}, f32[3,1024]{1,0:T(4,128)}, f32[3,1024]{1,0:T(4,128)}, f32[4,2,64]{2,1,0:T(2,128)}) custom-call(f32[19,2,64,128]{3,2,1,0:T(8,128)S(1)} %get-tuple-element.8.refs_0_, f32[3,1024]{1,0:T(4,128)S(1)} %get-tuple-element.9.refs_1_, f32[3,1024]{1,0:T(4,128)S(1)} %get-tuple-element.10.refs_2_, ...), custom_call_target="tpu_custom_call" | custom-call | tf_op jit(solution)/shard_map/put_out/pallas_call | solution.py:740

commit v4 on v3

--- a/solution.py
+++ b/solution.py
@@ -35,6 +35,7 @@
 ]
 DIRS = [lattice_dirs[i] for i in ORDER]
 FACES = [[p for p in range(19) if DIRS[p][0] == 1], [p for p in range(19) if DIRS[p][0] == -1]]
+STEEP = [[DIRS.index((0, y, z)) for y in (0, 1, -1)] for z in (1, -1)]
 velocity_scale = 10.0
 pair_strength = 0.5
 friction = 2.0
@@ -74,6 +75,25 @@
         plus = total_of(f[p] for p in range(19) if DIRS[p][axis] == 1)
         minus = total_of(f[p] for p in range(19) if DIRS[p][axis] == -1)
         vel.append((plus - minus) * inverse)
+    return density, vel
+
+
+def merged_fields(f, merged):
+    steep = [p for side in merged for p in STEEP[side]]
+    rest = [p for p in range(19) if p not in steep]
+    sums = {side: f[5 * side + 2] for side in merged}
+    density = total_of([f[p] for p in rest] + list(sums.values()))
+    inverse = 1.0 / density
+    vel = []
+    for axis in range(3):
+        plus = [f[p] for p in rest if DIRS[p][axis] == 1]
+        minus = [f[p] for p in rest if DIRS[p][axis] == -1]
+        if axis == 1:
+            plus += [f[5 * side + 3] for side in merged]
+        if axis == 2:
+            for side in merged:
+                (minus if side else plus).append(sums[side])
+        vel.append((total_of(plus) - total_of(minus)) * inverse)
     return density, vel
 
 
@@ -161,6 +181,7 @@
     blocks_in,
     send,
     recv,
+    late,
     swap_send,
     swap_recv,
 ):
@@ -228,9 +249,20 @@
     def collide_chunk(step, z, part):
         for x0 in range(*parts[part], 8):
             done = collided(load(step, z, x0), relax_ref[z, pl.ds(x0, 8), :])
-            for p, c in enumerate(DIRS):
-                value = done[p] if c[1] == 0 else pltpu.roll(done[p], c[1] % ny, axis=1)
-                post[step, p, z + 1, pl.ds(x0 + 8, 8), :] = value
+            done = [
+                done[p] if c[1] == 0 else pltpu.roll(done[p], c[1] % ny, axis=1)
+                for p, c in enumerate(DIRS)
+            ]
+            for side, edge in enumerate((top_z, 0)):
+                if step == LB_STEPS - 1 and z == edge:
+                    straight, ahead, back = (done[p] for p in STEEP[side])
+                    done[5 * side + 2 : 5 * side + 5] = [
+                        straight + (ahead + back),
+                        ahead - back,
+                        straight,
+                    ]
+            for p in range(19):
+                post[step, p, z + 1, pl.ds(x0 + 8, 8), :] = done[p]
 
     def copy(step, kind, slot, src, dst, peer):
         pltpu.make_async_remote_copy(
@@ -293,12 +325,12 @@
 
     def send_plane(step, rising, part):
         z, slot, peer = (top_z, 0, above) if rising else (0, cz + 1, below)
-        span = pl.ds(0 if rising else 5, 5)
+        span = pl.ds(0 if rising else 5, 4 if step == LB_STEPS - 1 else 5)
         low, high = parts[part]
         here = pl.ds(8 + low, high - low)
         copy(
             step,
-            2,
+            3 if step == LB_STEPS - 1 else 2,
             4 + part,
             post.at[step, span, z + 1, here, :],
             post.at[step, span, slot, here, :],
@@ -321,7 +353,8 @@
         for other, (first, last) in enumerate(parts):
             if first <= high and last >= low:
                 here = pl.ds(8 + first, last - first)
-                arrive(step, 4 + other, post.at[step, pl.ds(0, 10), 0, here, :])
+                span = pl.ds(0, 8 if step == LB_STEPS - 1 else 10)
+                arrive(step, 4 + other, post.at[step, span, 0, here, :])
 
     def send_chunk(step, rising, part):
         z = top_z if rising else 0
@@ -563,14 +596,44 @@
     for step in range(3, LB_STEPS):
         lattice_step(step)
 
+    def merged_of(z):
+        return [side for side, edge in enumerate((0, top_z)) if z == edge]
+
     def finish_chunk(z, part):
         for x0 in range(*parts[part], 8):
-            f = load(LB_STEPS, z, x0)
-            for p in range(19):
-                out_ref[ORDER[p], z, pl.ds(x0, 8), :] = f[p]
-            density, vel = fields(f)
+            density, vel = merged_fields(load(LB_STEPS, z, x0), merged_of(z))
             for c, value in enumerate((*vel, density)):
                 mean_ref[c, pl.ds(x0 + z * cx, 8), :] = value
+
+    late_part = post.at[LB_STEPS - 1, pl.ds(0, 2), 0, pl.ds(8, cx), :]
+
+    def send_rest():
+        for rising in (True, False):
+            z, slot, peer = (top_z, 0, above) if rising else (0, cz + 1, below)
+            here = (LB_STEPS - 1, 4 if rising else 9)
+            pltpu.make_async_remote_copy(
+                src_ref=post.at[here[0], here[1], z + 1, pl.ds(8, cx), :],
+                dst_ref=post.at[here[0], here[1], slot, pl.ds(8, cx), :],
+                send_sem=late.at[0],
+                recv_sem=late.at[1],
+                device_id=(peer, md),
+                device_id_type=MESH,
+            ).start()
+
+    def put_populations():
+        whole(late_part, late_part, late.at[0], late.at[1]).wait_recv()
+        for z in range(cz):
+            for x0 in range(0, cx, 8):
+                f = load(LB_STEPS, z, x0)
+                for side in merged_of(z):
+                    both, apart, straight = f[5 * side + 2 : 5 * side + 5]
+                    both = both - straight
+                    values = (straight, 0.5 * (both + apart), 0.5 * (both - apart))
+                    for p, value in zip(STEEP[side], values):
+                        f[p] = value
+                for p in range(19):
+                    out_ref[ORDER[p], z, pl.ds(x0, 8), :] = f[p]
+        whole(late_part, late_part, late.at[0], late.at[1]).wait_send()
 
     for part in range(chunks):
         with mark("need_last"):
@@ -589,9 +652,14 @@
         sums = by_hits(tgt[...], placed[...], ((1,), (1,)))
 
     def lattice_sent():
-        planes = post.at[:, pl.ds(0, 10), 0, pl.ds(8, cx), :]
-        for kind, ref in enumerate((rows_out, edge_out, planes)):
+        send_rest()
+        for kind, ref in enumerate((rows_out, edge_out)):
             whole(ref, ref, send.at[kind], recv.at[0, 0]).wait_send()
+        last = LB_STEPS - 1
+        earlier = post.at[pl.ds(0, last), pl.ds(0, 10), 0, pl.ds(8, cx), :]
+        whole(earlier, earlier, send.at[2], recv.at[0, 0]).wait_send()
+        latest = post.at[last, pl.ds(0, 8), 0, pl.ds(8, cx), :]
+        whole(latest, latest, send.at[3], recv.at[0, 0]).wait_send()
 
     with mark("swap0"):
         lines, blocks, sent_first = swap(0, sums[0:4] + sums[4:8] + sums[8:12], lattice_sent)
@@ -637,6 +705,7 @@
         moments = (sums[0:4] + sums[4:8] + sums[8:12]) / jnp.maximum(sums[12:13], 1.0)
 
     def put_particles():
+        put_populations()
         sent_first()
         for g in range(groups):
             here = pl.ds(g * 128, 128)
@@ -727,8 +796,9 @@
             pltpu.VMEM((16, slots), jnp.float32),
             pltpu.VMEM((2, devices, 1, 128), jnp.float32),
             pltpu.VMEM((2, devices, 1, 128), jnp.float32),
-            dma((3,)),
+            dma((4,)),
             dma((2, 4 + chunks)),
+            dma((2,)),
             dma((2,)),
             dma((2,)),
         ],

time: 52.7 us -> 51.6 us (0.979)
  Pallas kernels: 51.9 us -> 50.8 us
    pallas_call x1, Pallas kernels: 50.9 us -> 49.7 us  [on_device(): pl.pallas_call(functools.partial(coupled_kernel, n_slab, n_md), out_shape...]
where the time goes in v4:
time: 51.6 us; the launch traced here: 51.4 us
  Pallas kernels  50.8 us (98%)
  between operations  0.64 us (1%)
    pallas_call x1, Pallas kernels, on_device(): pl.pallas_call(functools.partial(coupled_kernel, n_slab, n_md), out_shape...  49.7 us
    pallas_call x1, Pallas kernels, on_device(): pl.pallas_call(put_out, out_shape=tuple((jax.ShapeDtypeStruct(shape, jnp....  1.08 us

profile of v4, /device:TPU:0, one launch (start us, length us, event | category | flops | bytes accessed | tf_op | source)
XLA Modules:
  0.0 51.4 jit_solution(14438502930270958180)
XLA Ops:
  0.6 49.7 %coupled.1 = (f32[19,2,64,128]{3,2,1,0:T(8,128)S(1)}, f32[3,1024]{1,0:T(4,128)S(1)}, f32[3,1024]{1,0:T(4,128)S(1)}, f32[4,2,64]{2,1,0:T(2,128)S(1)}) custom-call(f32[19,2,64,128]{3,2,1,0:T(8,128)} %f_hbm.1, f32[2,64,128]{2,1,0:T(8,128)} %relax_hbm.1, s32[2,2,64]{2,1,0:T(2,128)} %bitcast.5, f32[3,1024]{1,0:T(4,128)} %pos_hbm.1, f32[3,1024]{1,0:T(4,128)} %vel_hbm.1, ...), custom_call_target="tpu_custom_call" | custom-call | tf_op jit(solution)/shard_map/coupled/pallas_call | solution.py:767
  50.4 1.1 %put_out.1 = (f32[19,2,64,128]{3,2,1,0:T(8,128)}, f32[3,1024]{1,0:T(4,128)}, f32[3,1024]{1,0:T(4,128)}, f32[4,2,64]{2,1,0:T(2,128)}) custom-call(f32[19,2,64,128]{3,2,1,0:T(8,128)S(1)} %get-tuple-element.8.refs_0_, f32[3,1024]{1,0:T(4,128)S(1)} %get-tuple-element.9.refs_1_, f32[3,1024]{1,0:T(4,128)S(1)} %get-tuple-element.10.refs_2_, ...), custom_call_target="tpu_custom_call" | custom-call | tf_op jit(solution)/shard_map/put_out/pallas_call | solution.py:810

commit v5 on v4

--- a/solution.py
+++ b/solution.py
@@ -182,6 +182,7 @@
     send,
     recv,
     late,
+    apart,
     swap_send,
     swap_recv,
 ):
@@ -227,13 +228,24 @@
             f_parts.append(fetch(f_hbm.at[:, :, here, :], f_ref.at[:, :, here, :]))
         if len(f_parts) == 1:
             relax_part = fetch(relax_hbm, relax_ref)
-    if max(n_slab // 2, n_md // 2) <= LB_STEPS:
-        near = {(a % n_slab) * n_md + b % n_md for a in (-1, 0, 1) for b in (-1, 0, 1)}
-        greeted = sorted(near - {0})
+    reach = min(n_slab, n_md) > 2 and max(n_slab // 2, n_md // 2) <= LB_STEPS
+    first_slab, last_slab = slab == 0, slab == n_slab - 1
+
+    def signal(k, flag):
+        pl.semaphore_signal(flag, inc=1, device_id=peer_of(k), device_id_type=MESH)
+
+    if reach:
+        sides = [b % n_md for b in (0, 1, -1)]
+        for k in [n_md * (n_slab - 1) + b for b in sides] + sides[1:]:
+            signal(k, barrier)
+
+        @pl.when(jnp.logical_not(last_slab))
+        def _():
+            for b in sides:
+                signal(n_md + b, barrier)
     else:
-        greeted = list(range(1, devices))
-    for k in greeted:
-        pl.semaphore_signal(barrier, inc=1, device_id=peer_of(k), device_id_type=MESH)
+        for k in range(1, devices):
+            signal(k, barrier)
     pos_parts = [fetch(pos_hbm, pos_ref), fetch(vel_hbm, vel_ref), fetch(nbr_hbm, nbr_ref)]
     slots_part = fetch(slots_hbm, slots_ref)
     own_part = fetch(own_hbm, own_ref)
@@ -356,13 +368,32 @@
                 span = pl.ds(0, 8 if step == LB_STEPS - 1 else 10)
                 arrive(step, 4 + other, post.at[step, span, 0, here, :])
 
-    def send_chunk(step, rising, part):
-        z = top_z if rising else 0
+    def save_faces(step, z, part):
         for side in range(2):
             if part == outer[1 - side]:
                 save_face(step, z, side)
+
+    def send_blocks(step, rising, part):
+        for side in range(2):
+            if part == outer[1 - side]:
                 send_edge(step, rising, side)
         send_plane(step, rising, part)
+
+    def send_chunk(step, rising, part):
+        save_faces(step, top_z if rising else 0, part)
+        send_blocks(step, rising, part)
+
+    def send_first(rising, part):
+        save_faces(0, top_z if rising else 0, part)
+        if rising or not reach:
+            send_blocks(0, rising, part)
+        else:
+            pl.when(jnp.logical_not(first_slab))(lambda: send_blocks(0, rising, part))
+
+    def send_late_falling():
+        pl.semaphore_wait(apart, 3)
+        for part in range(chunks):
+            send_blocks(0, False, part)
 
     def lattice_step(step):
         for part in range(chunks):
@@ -377,8 +408,10 @@
             for rising in (True, False):
                 with mark("collide"):
                     collide_chunk(step, top_z if rising else 0, part)
-                if step or part:
+                if step:
                     send_chunk(step, rising, part)
+                elif part:
+                    send_first(rising, part)
             for z in range(1, top_z):
                 collide_chunk(step, z, part)
                 for side in range(2):
@@ -386,9 +419,17 @@
                         save_face(step, z, side)
             if step == 0 and part == 0:
                 with mark("barrier"):
-                    pl.semaphore_wait(barrier, len(greeted))
+                    expected = jnp.where(first_slab, 5, 8) if reach else devices - 1
+                    pl.semaphore_wait(barrier, expected)
+                if reach:
+
+                    @pl.when(last_slab)
+                    def _():
+                        for b in sides:
+                            signal(n_md + b, apart)
+
                 for rising in (True, False):
-                    send_chunk(step, rising, part)
+                    send_first(rising, part)
             for side in range(2):
                 if part == outer[1 - side]:
                     send_face(step, side)
@@ -585,6 +626,9 @@
         return lines, blocks, everyone.wait_send
 
     lattice_step(0)
+    if reach:
+        with mark("apart"):
+            pl.when(first_slab)(send_late_falling)
     with mark("prep_part"):
         prepare_particles()
     lattice_step(1)
@@ -799,6 +843,7 @@
             dma((4,)),
             dma((2, 4 + chunks)),
             dma((2,)),
+            pltpu.SemaphoreType.REGULAR,
             dma((2,)),
             dma((2,)),
         ],

time: 51.6 us -> 51.5 us (level)
  no operation moved by 1% of the time
where the time goes in v5:
time: 51.5 us; the launch traced here: 51.4 us
  Pallas kernels  50.7 us (98%)
  between operations  0.64 us (1%)
    pallas_call x1, Pallas kernels, on_device(): pl.pallas_call(functools.partial(coupled_kernel, n_slab, n_md), out_shape...  49.6 us
    pallas_call x1, Pallas kernels, on_device(): pl.pallas_call(put_out, out_shape=tuple((jax.ShapeDtypeStruct(shape, jnp....  1.08 us

profile of v5, /device:TPU:0, one launch (start us, length us, event | category | flops | bytes accessed | tf_op | source)
XLA Modules:
  0.0 51.4 jit_solution(7350845837846931996)
XLA Ops:
  0.6 49.6 %coupled.1 = (f32[19,2,64,128]{3,2,1,0:T(8,128)S(1)}, f32[3,1024]{1,0:T(4,128)S(1)}, f32[3,1024]{1,0:T(4,128)S(1)}, f32[4,2,64]{2,1,0:T(2,128)S(1)}) custom-call(f32[19,2,64,128]{3,2,1,0:T(8,128)} %f_hbm.1, f32[2,64,128]{2,1,0:T(8,128)} %relax_hbm.1, s32[2,2,64]{2,1,0:T(2,128)} %bitcast.5, f32[3,1024]{1,0:T(4,128)} %pos_hbm.1, f32[3,1024]{1,0:T(4,128)} %vel_hbm.1, ...), custom_call_target="tpu_custom_call" | custom-call | tf_op jit(solution)/shard_map/coupled/pallas_call | solution.py:811
  50.3 1.1 %put_out.1 = (f32[19,2,64,128]{3,2,1,0:T(8,128)}, f32[3,1024]{1,0:T(4,128)}, f32[3,1024]{1,0:T(4,128)}, f32[4,2,64]{2,1,0:T(2,128)}) custom-call(f32[19,2,64,128]{3,2,1,0:T(8,128)S(1)} %get-tuple-element.8.refs_0_, f32[3,1024]{1,0:T(4,128)S(1)} %get-tuple-element.9.refs_1_, f32[3,1024]{1,0:T(4,128)S(1)} %get-tuple-element.10.refs_2_, ...), custom_call_target="tpu_custom_call" | custom-call | tf_op jit(solution)/shard_map/put_out/pallas_call | solution.py:855
